TPU v7x, 512 devices: a 8x2x16 block of a 8x8x16 slice. The times are simulated.
512 devices in a mesh: groups: 2 (over y), seq: 16 (over z), heads: 8 (over x), sub: 2 (over core).
Axes of the slice: x: 8, y: 2, z: 16, core: 2. Of those that a mesh axis runs over, the one named last changes fastest.
The devices are a block of a 8x8x16 slice.
Arguments:
- queries: bfloat16 [8192, 8192], P(('groups', 'seq', 'sub'), 'heads'), parts along dimension 0, may hold values from -400 to 400
- keys: bfloat16 [8192, 1024], P(('groups', 'seq', 'sub'), 'heads'), parts along dimension 0, may hold values from -6 to 6
- values: bfloat16 [8192, 1024], P(('groups', 'seq', 'sub'), 'heads'), parts along dimension 0, may hold values from -18 to 18
- half_order: int32 [128], P('groups'), parts along dimension 0, may hold values from 0 to 63, as said below
- frame_lengths: int32 [64], P('groups'), parts along dimension 0, may hold values from 1 to 256, 4096 in all
- out_proj: bfloat16 [8192, 4096], P('heads', ('seq', 'sub')), may hold values from -0.125 to 0.125
- residual_in: bfloat16 [8192, 4096], P(('groups', 'seq', 'sub'), 'heads'), parts along dimension 0, may hold values from -40 to 40
- norm_gain: float32 [4096], P('heads'), may hold values from 0.5 to 1.5
Outputs:
- attended: bfloat16 [8192, 8192], P(('groups', 'seq', 'sub'), 'heads'), parts along dimension 0
- hidden_state: bfloat16 [8192, 4096], P(('groups', 'seq', 'sub'), 'heads'), parts along dimension 0
- normed: bfloat16 [8192, 4096], P(('groups', 'seq', 'sub'), 'heads'), parts along dimension 0
There are 2 independent parts, one for each index of `groups`. A program takes and returns all parts, laid end to end along the dimension named above; an argument that names none is the same for every part. Nothing has to cross between parts.
Inputs may be any that keep to these rules, and one draw needn't show every extreme that they name: `half_order`: a permutation of 0 to 63.
All inputs are finite; a program needn't handle non-finite values.
Results may differ from a plain program's by a relative error of at most 0.005.
Values may be sent and summed in bfloat16 or wider, within the bound.
No kernel may reach another device: no remote copies, remote signals or barrier semaphores. Data moves between devices by JAX's collectives and lax.ppermute only.
A program may use at most 64 MiB of HBM per device.

v0:
```python
import jax
import jax.numpy as jnp
from jax import lax
from jax.sharding import PartitionSpec as P

HEAD_WIDTH = 128
OUT_WIDTH = 4096


def side_by_side(arrays, axis, dim, along):
    ends, at = ([], 0)
    for a in arrays[:-1]:
        at += a.shape[along]
        ends.append(at)
    both = jnp.concatenate(arrays, axis=along)
    return tuple(jnp.split(lax.all_gather(both, axis, axis=dim, tiled=True), ends, axis=along))


def split_up(value, dim, devices):
    shape = value.shape
    parts = value.reshape(*shape[:dim], devices, shape[dim] // devices, *shape[dim + 1 :])
    return jnp.moveaxis(parts, dim, 0)


def summed_on_arrival(value, axis, dim):
    devices = lax.axis_size(axis)
    parts = lax.all_to_all(split_up(value, dim, devices), axis, 0, 0, tiled=True)
    return jnp.sum(parts.astype(jnp.float32), axis=0)


def from_everyone(value, axis):
    copies = jnp.broadcast_to(value, (lax.axis_size(axis), *value.shape))
    return lax.all_to_all(copies, axis, split_axis=0, concat_axis=0, tiled=True)


def of_everyone(value, axis):
    return from_everyone(value, axis).sum(axis=0)


def shards(queries, keys, values, half_order, frame_lengths, out_proj, residual_in, norm_gain):
    tok_rows = queries.shape[0]
    kv_local = keys.shape[1] // HEAD_WIDTH
    group_width = queries.shape[1] // keys.shape[1]
    half_rows = tok_rows // 2
    own_index = lax.axis_index("seq") * lax.axis_size("sub") + lax.axis_index("sub")
    table_ids = jnp.arange(half_order.shape[0], dtype=jnp.int32)

    def locate(row_ids):
        matches = (row_ids // half_rows)[:, None] == table_ids[None, :]
        offsets = jnp.sum(jnp.where(matches, half_order[None, :], 0), axis=1)
        return offsets * half_rows + row_ids % half_rows

    query_pos = locate(own_index * tok_rows + jnp.arange(tok_rows, dtype=jnp.int32))
    frame_ends = jnp.cumsum(frame_lengths)
    frame_starts = frame_ends - frame_lengths
    frame_limit = jnp.sum(
        jnp.where(frame_starts[None, :] <= query_pos[:, None], frame_lengths[None, :], 0), axis=1
    )
    query_head_rows = queries.reshape(tok_rows, kv_local, group_width, HEAD_WIDTH)
    score_scale = HEAD_WIDTH ** (-0.5)
    initial = (
        jnp.full((kv_local, group_width, tok_rows), -1e30, jnp.float32),
        jnp.zeros((kv_local, group_width, tok_rows), jnp.float32),
        jnp.zeros((kv_local, group_width, tok_rows, HEAD_WIDTH), jnp.float32),
    )
    key_piece, value_piece = side_by_side((keys, values), ("seq", "sub"), 0, 1)
    piece_rows = key_piece.shape[0]
    key_pos = locate(jnp.arange(piece_rows, dtype=jnp.int32))

    def absorb_piece(current):
        running_max, denominator, numerator = current
        key_view = key_piece.reshape(piece_rows, kv_local, HEAD_WIDTH)
        value_view = value_piece.reshape(piece_rows, kv_local, HEAD_WIDTH)
        scores = (
            jnp.einsum(
                "qhgd,khd->hgqk", query_head_rows, key_view, preferred_element_type=jnp.float32
            )
            * score_scale
        )
        visible = key_pos[None, :] < frame_limit[:, None]
        scores = jnp.where(visible, scores, -1e30)
        new_max = jnp.maximum(running_max, jnp.max(scores, axis=-1))
        weights = jnp.where(visible, jnp.exp(scores - new_max[..., None]), 0.0)
        denominator = jnp.sum(weights, axis=-1)
        product = jnp.einsum(
            "hgqk,khd->hgqd",
            weights.astype(jnp.bfloat16),
            value_view,
            preferred_element_type=jnp.float32,
        )
        numerator = product
        return (new_max, denominator, numerator)

    running_max, denominator, numerator = lax.cond(
        jnp.min(key_pos) < jnp.max(frame_limit), absorb_piece, lambda current: current, initial
    )
    result = numerator / denominator[..., None]
    attended = (
        jnp.transpose(result, (2, 0, 1, 3))
        .reshape(tok_rows, kv_local * group_width * HEAD_WIDTH)
        .astype(jnp.bfloat16)
    )
    head_terms = jnp.dot(
        attended,
        lax.all_gather(out_proj, ("seq", "sub"), axis=1, tiled=True),
        preferred_element_type=jnp.float32,
    )
    projected = summed_on_arrival(head_terms.astype(jnp.bfloat16), "heads", 1)
    hidden_state = (residual_in.astype(jnp.float32) + projected).astype(jnp.bfloat16)
    widened = hidden_state.astype(jnp.float32)
    energy = of_everyone(jnp.sum(widened * widened, axis=1), "heads") / OUT_WIDTH
    normed = (widened * lax.rsqrt(energy + 1e-06)[:, None] * norm_gain[None, :]).astype(
        jnp.bfloat16
    )
    return (attended, hidden_state, normed)


def solution(mesh):
    in_specs = (
        P(("groups", "seq", "sub"), "heads"),
        P(("groups", "seq", "sub"), "heads"),
        P(("groups", "seq", "sub"), "heads"),
        P("groups"),
        P("groups"),
        P("heads", ("seq", "sub")),
        P(("groups", "seq", "sub"), "heads"),
        P("heads"),
    )
    out_specs = (
        P(("groups", "seq", "sub"), "heads"),
        P(("groups", "seq", "sub"), "heads"),
        P(("groups", "seq", "sub"), "heads"),
    )
    return jax.shard_map(shards, mesh=mesh, in_specs=in_specs, out_specs=out_specs, check_vma=False)
```

profile of v0, /device:TPU:80, one launch (start us, length us, event | category | flops | bytes accessed | tf_op | source)
XLA Modules:
  0.0 271.7 jit_solution(6806642003269453513)
XLA Ops:
  7.2 0.1 all-gather.3.cloned.1.call-start
  7.2 1.4 pad_maximum_fusion
  8.7 0.1 all-gather.3.cloned.1.call-update
  8.7 0.1 all-gather.5.cloned.1.call-start
  8.8 0.7 all-gather.5.cloned.1.call-update
  9.5 0.7 copy.32
  10.3 0.1 reduce-window.9
  10.3 0.1 reduce.3
  10.5 0.7 sub.24
  11.1 0.7 select_reduce_fusion.1
  11.9 0.7 select_reduce_fusion.2
  12.6 0.6 reduce_max.18
  13.3 0.9 select_reduce_fusion
  14.2 0.6 fusion.33
  16.1 100.8 %all-gather.3.cloned.1.call-done = bf16[4096,256]{1,0:T(8,128)(2,1)} async-done(((bf16[128,256]{1,0:T(8,128)(2,1)}), bf16[4096,256]{1,0:T(8,128)(2,1)}) %all-gather.3.cloned.1.call-update) | async-done | bytes 2097168 | tf_op jit(solution)/shard_map/all_gather | solution.py:16
  116.9 14.2 %conditional.1 = (f32[1,8,128]{2,1,0:T(8,128)S(1)}, f32[1,8,128,128]{3,2,1,0:T(8,128)S(1)}) conditional(s32[]{:T(128)} %convert_element_type.33, () %tuple.16, (s32[4096]{0:T(1024)S(1)}, s32[128]{0:T(128)S(1)}, bf16[4096,256]{1,0:T(8,128)(2,1)}, bf16[128,1024]{1,0:T(8,128)(2,1)}) %tuple.17), branch_computations={%region_6.7_spmd, %region_7.10_spmd} | conditional | flops 2202532864 | bytes 63742508 | solution.py:94
  116.9 1.8 broadcast_compare_fusion
  118.7 3.8 %fusion = (f32[8,128]{1,0:T(8,128)S(1)}, f32[4096,128,8]{1,0,2:T(8,128)S(1)}) fusion(pred[128,4096]{0,1:T(8,128)(4,1)S(1)} %broadcast_compare_fusion, bf16[4096,256]{1,0:T(8,128)(2,1)} %get-tuple-element.14, bf16[128,1024]{1,0:T(8,128)(2,1)} %get-tuple-element.24), kind=kOutput, calls=%fused_computation.2 | convolution fusion | flops 1086323712 | bytes 18616320 | tf_op jit(solution)/shard_map/cond/branch_1_fun/qhgd,khd->hgqk/dot_general | solution.py:75
  122.6 4.4 %fusion.7 = f32[1,8,128,128]{3,2,1,0:T(8,128)S(1)} fusion(f32[4096,128,8]{1,0,2:T(8,128)S(1)} %get-tuple-element.30, f32[8,128]{1,0:T(8,128)S(1)} %broadcast_maximum_fusion, pred[128,4096]{0,1:T(8,128)(4,1)S(1)} %broadcast_compare_fusion, bf16[4096,256]{1,0:T(8,128)(2,1)S(1)} %copy-done.4), kind=kOutput, calls=%fused_computation.8 | convolution fusion | flops 1094713344 | bytes 18878464 | tf_op jit(solution)/shard_map/cond/branch_1_fun/hgqk,khd->hgqd/dot_general | solution.py:85
  127.0 4.0 %fusion.2 = f32[8,128]{1,0:T(8,128)S(1)} fusion(f32[4096,128,8]{1,0,2:T(8,128)S(1)} %get-tuple-element.30, f32[8,128]{1,0:T(8,128)S(1)} %broadcast_maximum_fusion, pred[128,4096]{0,1:T(8,128)(4,1)S(1)} %broadcast_compare_fusion), kind=kLoop, calls=%fused_computation.4 | loop fusion | flops 20970496 | bytes 17309696 | tf_op jit(solution)/shard_map/cond/branch_1_fun/reduce_sum | solution.py:84
  131.1 0.0 copy-start.2
  131.1 0.2 fusion.23
  131.3 0.2 copy.33
  131.5 0.0 copy-start
  131.6 81.7 %all-gather.5.cloned.1.call-done = bf16[1024,4096]{1,0:T(8,128)(2,1)} async-done(((bf16[1024,128]{1,0:T(8,128)(2,1)}), bf16[1024,4096]{1,0:T(8,128)(2,1)}) %all-gather.5.cloned.1.call-update) | async-done | bytes 8388624 | tf_op jit(solution)/shard_map/all_gather | solution.py:105
  213.2 4.6 %convolution_convert_fusion = bf16[128,4096]{1,0:T(8,128)(2,1)S(1)} fusion(bf16[128,1024]{1,0:T(8,128)(2,1)S(1)} %bitcast.64, bf16[1024,4096]{1,0:T(8,128)(2,1)} %all-gather.5.cloned.1.call-done), kind=kOutput, calls=%fused_computation.21 | convolution fusion | flops 1074266112 | bytes 9699328 | tf_op jit(solution)/shard_map/dot_general | solution.py:103
  217.9 0.1 copy.48
  218.0 35.6 %all_to_all.11 = bf16[8,128,512]{2,1,0:T(8,128)(2,1)S(1)} all-to-all(bf16[8,128,512]{2,1,0:T(8,128)(2,1)S(1)} %bitcast.62), channel_id=1, replica_groups=mesh['groups'=2,'seq'=16,'heads'=8,'sub'=2] {'heads'}, dimensions={0} | all-to-all | bytes 2097152 | tf_op jit(solution)/shard_map/all_to_all | solution.py:27
  253.6 0.1 convert_reduce_fusion
  253.8 0.1 fusion.20
  253.9 10.1 %all_to_all.12 = f32[8,1,128]{2,1,0:T(1,128)S(1)} all-to-all(f32[8,1,128]{2,1,0:T(1,128)S(1)} %broadcast_in_dim.81), channel_id=1, replica_groups=mesh['groups'=2,'seq'=16,'heads'=8,'sub'=2] {'heads'}, dimensions={0} | all-to-all | bytes 8192 | tf_op jit(solution)/shard_map/all_to_all | solution.py:33
  264.0 0.8 fusion.22
  (16 shorter events, 0.1 us)
Async XLA Ops:
  7.2 109.7 %all-gather.3.cloned.1.call-start = ((), (), s32[]{:S(2)}) async-start(), calls=%async_computation.2 | async-start | bytes 2162688 | tf_op jit(solution)/shard_map/all_gather | solution.py:16
  8.7 204.5 %all-gather.5.cloned.1.call-start = ((), (), s32[]{:S(2)}) async-start(), calls=%async_computation.3 | async-start | bytes 8650752 | tf_op jit(solution)/shard_map/all_gather | solution.py:105
  116.9 5.7 %copy-start.4 = (bf16[4096,256]{1,0:T(8,128)(2,1)S(1)}, bf16[4096,256]{1,0:T(8,128)(2,1)}, u32[]{:S(2)}) copy-start(bf16[4096,256]{1,0:T(8,128)(2,1)} %get-tuple-element.14) | copy-start | bytes 6291460 | tf_op jit(solution)/shard_map/cond
  131.1 122.7 %copy-start.2 = (bf16[128,512]{1,0:T(8,128)(2,1)S(1)}, bf16[128,512]{1,0:T(8,128)(2,1)}, u32[]{:S(2)}) copy-start(bf16[128,512]{1,0:T(8,128)(2,1)} %param.16) | copy-start | bytes 393220
  131.1 133.0 %copy-start.3 = (f32[512]{0:T(512)S(1)}, f32[512]{0:T(512)}, u32[]{:S(2)}) copy-start(f32[512]{0:T(512)} %param.17) | copy-start | bytes 6148
  131.5 133.3 %copy-start = (bf16[16,8,8,128]{3,1,2,0:T(8,128)(2,1)}, bf16[16,8,8,128]{3,1,2,0:T(8,128)(2,1)S(1)}, u32[]{:S(2)}) copy-start(bf16[16,8,8,128]{3,1,2,0:T(8,128)(2,1)S(1)} %copy.49) | copy-start | bytes 786436
  253.9 10.9 %copy-start.1 = (bf16[128,512]{1,0:T(8,128)(2,1)}, bf16[128,512]{1,0:T(8,128)(2,1)S(1)}, u32[]{:S(2)}) copy-start(bf16[128,512]{1,0:T(8,128)(2,1)S(1)} %get-tuple-element.26) | copy-start | bytes 393220
Sparse Core Ops, SparseCore 0:
  10.7 106.1 all-gather.2
  118.9 94.2 all-gather.4
where the time goes:
time: 272 us
  waiting for transfers between devices  183 us (67%)
  blocking collectives  45.8 us (17%)
  between operations  15.5 us (6%)
  other arithmetic  13.1 us (5%)
  matrix products  12.9 us (5%)
    all_gather x1, waiting for transfers between devices, side_by_side(): lax.all_gather(both, axis, axis=dim, tiled=True)  101 us
    all_gather x1, waiting for transfers between devices, shards(): lax.all_gather(out_proj, ('seq', 'sub'), axis=1, tiled=True)  81.7 us
    all_to_all x1, blocking collectives, summed_on_arrival(): lax.all_to_all(split_up(value, dim, devices), axis, 0, 0, tiled=True)  35.6 us
    all_to_all x1, blocking collectives, from_everyone(): return lax.all_to_all(copies, axis, split_axis=0, concat_axis=0, tiled=True)  10.1 us
  transfers between devices with their start and end apart: 2, of which 2 were waited for; matrix products, arithmetic and copies ran while one was open for 7% of the time, Pallas kernels for 0%

commit v1 on v0

v1 whole, which is shorter than its diff:
```python
import jax
import jax.numpy as jnp
from jax import lax
from jax.experimental import pallas as pl
from jax.experimental.pallas import tpu as pltpu
from jax.sharding import PartitionSpec as P

HEAD_WIDTH = 128
SCALE = HEAD_WIDTH ** (-0.5)


def swapped(value):
    return lax.ppermute(value, "sub", [(0, 1), (1, 0)])


def everyone_sum(value):
    copies = jnp.broadcast_to(value, (lax.axis_size("heads"), *value.shape))
    return lax.all_to_all(copies, "heads", split_axis=0, concat_axis=0, tiled=True).sum(axis=0)


def attend_kernel(q_ref, k_ref, v_ref, kv_ref, pos_ref, limit_ref, out_ref):
    own = k_ref.shape[0]
    keys = (k_ref[...], kv_ref[:own])
    values = (v_ref[...], kv_ref[own:])
    scores = []
    for j in range(2):
        part = lax.dot_general(
            q_ref[...], keys[j], (((1,), (1,)), ((), ())), preferred_element_type=jnp.float32
        )
        visible = pos_ref[:, j * own : (j + 1) * own] < limit_ref[...]
        scores.append(jnp.where(visible, part * SCALE, -1e30))
    row_max = jnp.maximum(
        jnp.max(scores[0], axis=-1, keepdims=True), jnp.max(scores[1], axis=-1, keepdims=True)
    )
    total, product = 0.0, 0.0
    for j in range(2):
        weights = jnp.exp(scores[j] - row_max)
        total += jnp.sum(weights, axis=-1, keepdims=True)
        product += jnp.dot(
            weights.astype(jnp.bfloat16), values[j], preferred_element_type=jnp.float32
        )
    out_ref[...] = (product / total).astype(out_ref.dtype)


def attend(queries, keys, values, kv_other, key_pos, limit):
    rows, width = queries.shape
    heads, count = width // HEAD_WIDTH, key_pos.shape[1]
    whole = lambda a: pl.BlockSpec(a.shape, lambda h: (0, 0))
    return pl.pallas_call(
        attend_kernel,
        grid=(heads,),
        in_specs=[
            pl.BlockSpec((rows, HEAD_WIDTH), lambda h: (0, h)),
            whole(keys),
            whole(values),
            whole(kv_other),
            whole(key_pos),
            whole(limit),
        ],
        out_specs=pl.BlockSpec((rows, HEAD_WIDTH), lambda h: (0, h)),
        out_shape=jax.ShapeDtypeStruct((rows, width), jnp.bfloat16),
        compiler_params=pltpu.CompilerParams(vmem_limit_bytes=24 << 20),
        cost_estimate=pl.CostEstimate(
            flops=4 * rows * width * count,
            bytes_accessed=4 * rows * width + 4 * count * HEAD_WIDTH,
            transcendentals=rows * heads * count,
        ),
    )(queries, keys, values, kv_other, key_pos, limit)


def project_kernel(a_ref, w_ref, out_ref):
    rows = out_ref.shape[2]
    wide = w_ref.shape[2]
    for j in range(w_ref.shape[0]):
        part = jnp.dot(a_ref[...], w_ref[j], preferred_element_type=jnp.float32)
        part = part.astype(jnp.bfloat16)
        for c in range(out_ref.shape[1]):
            out_ref[0, c, :, j * wide : (j + 1) * wide] = part[c * rows : (c + 1) * rows]


def project(both, weights, nx):
    chips, depth, wide = weights.shape
    rows, per = both.shape[0] // 2, chips // nx
    return pl.pallas_call(
        project_kernel,
        grid=(nx,),
        in_specs=[
            pl.BlockSpec(both.shape, lambda h: (0, 0)),
            pl.BlockSpec((per, depth, wide), lambda h: (h, 0, 0)),
        ],
        out_specs=pl.BlockSpec((1, 2, rows, per * wide), lambda h: (h, 0, 0, 0)),
        out_shape=jax.ShapeDtypeStruct((nx, 2, rows, per * wide), jnp.bfloat16),
        compiler_params=pltpu.CompilerParams(vmem_limit_bytes=16 << 20),
        cost_estimate=pl.CostEstimate(
            flops=4 * rows * depth * wide * chips,
            bytes_accessed=2 * weights.size,
            transcendentals=0,
        ),
    )(both, weights)


def shards(queries, keys, values, half_order, frame_lengths, out_proj, residual_in, norm_gain):
    tok_rows = queries.shape[0]
    half_rows = tok_rows // 2
    chips, nx = lax.axis_size("seq"), lax.axis_size("heads")
    z, core = lax.axis_index("seq"), lax.axis_index("sub")
    features = residual_in.shape[1] * nx

    weights = lax.all_gather(out_proj, "seq")
    k_own = lax.all_gather(keys, "seq", tiled=True)
    v_own = lax.all_gather(values, "seq", tiled=True)
    kv_other = swapped(jnp.concatenate([k_own, v_own], axis=0))

    inner = jnp.arange(half_rows, dtype=jnp.int32)
    table = (half_order[:, None] * half_rows + inner[None, :]).reshape(chips, 2, tok_rows)
    of_core = [table[:, 0].reshape(1, -1), table[:, 1].reshape(1, -1)]
    key_pos = jnp.where(
        core == 0,
        jnp.concatenate(of_core, axis=1),
        jnp.concatenate(of_core[::-1], axis=1),
    )
    chosen = (jnp.arange(2 * chips, dtype=jnp.int32) == 2 * z + core)[:, None]
    query_pos = jnp.sum(jnp.where(chosen, table.reshape(2 * chips, tok_rows), 0), axis=0)
    frame_starts = jnp.cumsum(frame_lengths) - frame_lengths
    limit = jnp.sum(
        jnp.where(frame_starts[None, :] <= query_pos[:, None], frame_lengths[None, :], 0), axis=1
    )[:, None]
    attended = attend(queries, k_own, v_own, kv_other, key_pos, limit)

    both = lax.all_gather(attended, "sub", tiled=True)
    parts = project(both, weights, nx)
    per = chips // nx
    parts = parts.reshape(2 * nx, tok_rows, -1)
    parts = lax.all_to_all(parts, ("heads", "sub"), 0, 0, tiled=True)
    parts = parts.reshape(nx, 2, tok_rows, per, -1)
    projected = jnp.sum(parts.astype(jnp.float32), axis=0)
    projected = jnp.transpose(projected, (1, 2, 0, 3)).reshape(tok_rows, -1)

    hidden_state = (residual_in.astype(jnp.float32) + projected).astype(jnp.bfloat16)
    widened = hidden_state.astype(jnp.float32)
    energy = everyone_sum(jnp.sum(widened * widened, axis=1)) / features
    normed = (widened * lax.rsqrt(energy + 1e-06)[:, None] * norm_gain[None, :]).astype(
        jnp.bfloat16
    )
    return (attended, hidden_state, normed)


def solution(mesh):
    rows = P(("groups", "seq", "sub"), "heads")
    in_specs = (rows, rows, rows, P("groups"), P("groups"), P("heads", ("seq", "sub")), rows, P("heads"))
    return jax.shard_map(
        shards, mesh=mesh, in_specs=in_specs, out_specs=(rows, rows, rows), check_vma=False
    )
```

time: 272 us -> 197 us (0.72)
  waiting for transfers between devices: 183 us -> 35 us
  blocking collectives: 45.8 us -> 109 us
  Pallas kernels: 0 us -> 15.6 us
  starting transfers between devices: 0.13 us -> 14.5 us
  matrix products: 12.9 us -> 0 us
  other arithmetic: 13.1 us -> 1.69 us
  local copies, waits for them, and re-layouts: 1.07 us -> 6.49 us
    all_gather x2 -> x1, waiting for transfers between devices: 182 us -> 0.01 us  [shards(): weights = lax.all_gather(out_proj, 'seq')]
    all_gather x0 -> x3, blocking collectives: none -> 109 us  [the longest x1 72.3 us: shards(): k_own = lax.all_gather(keys, 'seq', tiled=True)]
    all_to_all x2 -> x0, blocking collectives: 45.8 us -> none  [the longest x1 35.6 us: summed_on_arrival(): lax.all_to_all(split_up(value, dim, devices), axis, 0, 0, tiled=True)]
    all_to_all x0 -> x2, waiting for transfers between devices: none -> 33 us  [the longest x1 26.2 us: shards(): parts = lax.all_to_all(parts, ('heads', 'sub'), 0, 0, tiled=True)]
    pallas_call x0 -> x2, Pallas kernels: none -> 15.6 us  [the longest x1 10.8 us: attend(): pl.pallas_call(attend_kernel, grid=(heads,), in_specs=[pl.BlockSpec((rows...]
    dot_general x3 -> x0, matrix products: 12.9 us -> none  [the longest x1 4.64 us: shards(): jnp.dot(attended, lax.all_gather(out_proj, ('seq', 'sub'), axis=1, tiled=...]
    all_to_all x0 -> x2, starting transfers between devices: none -> 12.5 us  [the longest x1 7.67 us: shards(): parts = lax.all_to_all(parts, ('heads', 'sub'), 0, 0, tiled=True)]
    reduce_sum x6 -> x4, other arithmetic: 5.94 us -> 1.18 us  [the longest x1 0.97 us: shards(): projected = jnp.sum(parts.astype(jnp.float32), axis=0)]
  transfers between devices with their start and end apart: 2 -> 4, of which waited for: 2 -> 3; matrix products, arithmetic and copies ran while one was open for 7% -> 1% of each run, Pallas kernels for 0% -> 5%
where the time goes in v1:
time: 197 us; the launch traced here: 196 us
  blocking collectives  109 us (55%)
  waiting for transfers between devices  35 us (18%)
  Pallas kernels  15.6 us (8%)
  starting transfers between devices  14.5 us (7%)
  between operations  14.2 us (7%)
  local copies, waits for them, and re-layouts  6.49 us (3%)
    all_gather x1, blocking collectives, shards(): k_own = lax.all_gather(keys, 'seq', tiled=True)  72.3 us
    all_gather x1, blocking collectives, shards(): v_own = lax.all_gather(values, 'seq', tiled=True)  34.2 us
    all_to_all x1, waiting for transfers between devices, shards(): parts = lax.all_to_all(parts, ('heads', 'sub'), 0, 0, tiled=True)  26.2 us
    pallas_call x1, Pallas kernels, attend(): pl.pallas_call(attend_kernel, grid=(heads,), in_specs=[pl.BlockSpec((rows...  10.8 us
    all_to_all x1, starting transfers between devices, shards(): parts = lax.all_to_all(parts, ('heads', 'sub'), 0, 0, tiled=True)  7.67 us
    all_to_all x1, waiting for transfers between devices, everyone_sum(): lax.all_to_all(copies, 'heads', split_axis=0, concat_axis=0, tiled=True)  6.86 us
    all_to_all x1, starting transfers between devices, everyone_sum(): lax.all_to_all(copies, 'heads', split_axis=0, concat_axis=0, tiled=True)  4.84 us
    pallas_call x1, Pallas kernels, project(): pl.pallas_call(project_kernel, grid=(nx,), in_specs=[pl.BlockSpec(both.sh...  4.76 us
  transfers between devices with their start and end apart: 4, of which 3 were waited for; matrix products, arithmetic and copies ran while one was open for 1% of the time, Pallas kernels for 5%

profile of v1, /device:TPU:80, one launch (start us, length us, event | category | flops | bytes accessed | tf_op | source)
XLA Modules:
  0.0 196.5 jit_solution(16219104229808085648)
XLA Ops:
  7.3 0.7 all-gather.3.cloned.1.call-update
  8.0 72.3 %all_gather.15.k_ref = bf16[2048,128]{1,0:T(8,128)(2,1)S(1)} all-gather(bf16[128,128]{1,0:T(8,128)(2,1)} %param.9), channel_id=1, replica_groups=mesh['groups'=2,'seq'=16,'heads'=8,'sub'=2] {'seq'}, dimensions={0}, use_global_device_ids=true | all-gather | bytes 557056 | tf_op jit(solution)/shard_map/all_gather | solution.py:110
  80.3 34.2 %all_gather.16.v_ref = bf16[2048,128]{1,0:T(8,128)(2,1)S(1)} all-gather(bf16[128,128]{1,0:T(8,128)(2,1)} %param.10), channel_id=1, replica_groups=mesh['groups'=2,'seq'=16,'heads'=8,'sub'=2] {'seq'}, dimensions={0}, use_global_device_ids=true | all-gather | bytes 557056 | tf_op jit(solution)/shard_map/all_gather | solution.py:111
  114.6 2.0 collective-permute-start
  116.6 0.1 add.56
  116.8 0.1 select_reduce_fusion
  116.9 0.1 add.48
  117.1 0.1 add.49
  117.1 0.1 add.50
  117.2 0.1 add.52
  117.4 0.1 copy.36
  117.6 0.1 reduce.2
  117.7 0.1 select_reduce_fusion.1
  117.8 0.1 copy.38.limit_ref
  117.9 1.3 collective-permute-done.kv_ref
  119.2 10.8 %shard_map.103 = bf16[128,1024]{1,0:T(8,128)(2,1)} custom-call(bf16[128,1024]{1,0:T(8,128)(2,1)S(1)} %copy-done.1, bf16[2048,128]{1,0:T(8,128)(2,1)S(1)} %all_gather.15.k_ref, bf16[2048,128]{1,0:T(8,128)(2,1)S(1)} %all_gather.16.v_ref, bf16[4096,128]{1,0:T(8,128)(2,1)S(1)} %collective-permute-done.kv_ref, s32[1,4096]{1,0:T(1,128)S(1)} %broadcast_select_fusion.pos_ref, ...), custom_call_target="tpu_custom_call" | custom-call | flops 2147483648 | bytes 2621440 | tf_op jit(solution)/shard_map/pallas_call | solution.py:49
  130.0 2.4 %all_gather.17.a_ref = bf16[256,1024]{1,0:T(8,128)(2,1)S(1)} all-gather(bf16[128,1024]{1,0:T(8,128)(2,1)} %shard_map.103), channel_id=1, replica_groups=mesh['groups'=2,'seq'=16,'heads'=8,'sub'=2] {'sub'}, dimensions={0}, use_global_device_ids=true | all-gather | bytes 786432 | tf_op jit(solution)/shard_map/all_gather | solution.py:130
  132.4 2.2 %copy-done = bf16[16384,128]{1,0:T(8,128)(2,1)S(1)} copy-done((bf16[16384,128]{1,0:T(8,128)(2,1)S(1)}, bf16[16384,128]{1,0:T(8,128)(2,1)}, u32[]{:S(2)}) %copy-start) | copy-done | bytes 4194328
  134.6 4.8 %shard_map.104 = bf16[8,2,128,256]{3,2,1,0:T(8,128)(2,1)} custom-call(bf16[256,1024]{1,0:T(8,128)(2,1)S(1)} %all_gather.17.a_ref, bf16[16,1024,128]{2,1,0:T(8,128)(2,1)S(1)} %bitcast.15), custom_call_target="tpu_custom_call" | custom-call | flops 1073741824 | bytes 4194304 | tf_op jit(solution)/shard_map/pallas_call | solution.py:84
  139.4 7.7 %all-to-all-start = ((bf16[16,128,256]{2,1,0:T(8,128)(2,1)}), bf16[16,128,256]{2,1,0:T(8,128)(2,1)S(1)}, u32[]{:S(2)}, u32[]{:S(2)}) async-start(bf16[16,128,256]{2,1,0:T(8,128)(2,1)} %bitcast.5), calls=%async_computation | async-start | bytes 2097152 | tf_op jit(solution)/shard_map/all_to_all | solution.py:134
  147.1 0.1 copy.39
  147.2 26.2 %all-to-all-done = bf16[16,128,256]{2,1,0:T(8,128)(2,1)S(1)} async-done(((bf16[16,128,256]{2,1,0:T(8,128)(2,1)}), bf16[16,128,256]{2,1,0:T(8,128)(2,1)S(1)}, u32[]{:S(2)}, u32[]{:S(2)}) %all-to-all-start) | async-done | bytes 1048608 | tf_op jit(solution)/shard_map/all_to_all | solution.py:134
  173.3 1.0 reshape.152
  174.4 1.0 reduce_sum.47
  175.4 0.1 copy.40
  175.5 0.1 fusion
  175.6 0.6 broadcast_in_dim.43
  176.2 4.8 %all-to-all-start.1 = ((f32[8,1,128]{2,1,0:T(1,128)}), f32[8,1,128]{2,1,0:T(1,128)S(1)}, u32[]{:S(2)}, u32[]{:S(2)}) async-start(f32[8,1,128]{2,1,0:T(1,128)} %broadcast_in_dim.43), calls=%async_computation.1 | async-start | bytes 8192 | tf_op jit(solution)/shard_map/all_to_all | solution.py:18
  181.1 0.8 copy.42
  181.8 6.9 %all-to-all-done.1 = f32[8,1,128]{2,1,0:T(1,128)S(1)} async-done(((f32[8,1,128]{2,1,0:T(1,128)}), f32[8,1,128]{2,1,0:T(1,128)S(1)}, u32[]{:S(2)}, u32[]{:S(2)}) %all-to-all-start.1) | async-done | bytes 4128 | tf_op jit(solution)/shard_map/all_to_all | solution.py:18
  188.7 0.1 fusion.2
  188.9 0.8 copy.43
  (27 shorter events, 0.4 us)
Async XLA Ops:
  7.2 109.4 %copy-start.5 = (s32[64]{0:T(128)S(1)}, s32[64]{0:T(128)}, u32[]{:S(2)}) copy-start(s32[64]{0:T(128)} %param.11) | copy-start | bytes 772
  7.2 110.2 %copy-start.4 = (s32[32]{0:T(128)S(1)}, s32[32]{0:T(128)}, u32[]{:S(2)}) copy-start(s32[32]{0:T(128)} %param.12) | copy-start | bytes 388
  7.2 112.0 %copy-start.1 = (bf16[128,1024]{1,0:T(8,128)(2,1)S(1)}, bf16[128,1024]{1,0:T(8,128)(2,1)}, u32[]{:S(2)}) copy-start(bf16[128,1024]{1,0:T(8,128)(2,1)} %q_ref.1) | copy-start | bytes 786436
  7.2 125.2 %all-gather.3.cloned.1.call-start = ((), (), s32[]{:S(2)}) async-start(), calls=%async_computation.2 | async-start | bytes 4456448 | tf_op jit(solution)/shard_map/all_gather | solution.py:109
  114.6 4.6 %collective-permute-start = (bf16[4096,128]{1,0:T(8,128)(2,1)S(1)}, bf16[4096,128]{1,0:T(8,128)(2,1)S(1)}, u32[]{:S(2)}, u32[]{:S(2)}) collective-permute-start(bf16[4096,128]{1,0:T(8,128)(2,1)S(1)} %pad_maximum_fusion), channel_id=1, source_target_pairs={{0,1},{1,0},{2,3},{3,2},{4,5},{5,4},{6,7},{7,6},{8,9},{9,8},{10,11... | collective-permute-start | bytes 3145736 | tf_op jit(solution)/shard_map/ppermute | solution.py:13
  132.4 2.2 %copy-start = (bf16[16384,128]{1,0:T(8,128)(2,1)S(1)}, bf16[16384,128]{1,0:T(8,128)(2,1)}, u32[]{:S(2)}) copy-start(bf16[16384,128]{1,0:T(8,128)(2,1)} %all-gather.3.cloned.1.call-done) | copy-start | bytes 12582916
  139.4 7.7 %copy-start.2 = (bf16[128,512]{1,0:T(8,128)(2,1)S(1)}, bf16[128,512]{1,0:T(8,128)(2,1)}, u32[]{:S(2)}) copy-start(bf16[128,512]{1,0:T(8,128)(2,1)} %param.14) | copy-start | bytes 393220
  139.4 34.0 %all-to-all-start = ((bf16[16,128,256]{2,1,0:T(8,128)(2,1)}), bf16[16,128,256]{2,1,0:T(8,128)(2,1)S(1)}, u32[]{:S(2)}, u32[]{:S(2)}) async-start(bf16[16,128,256]{2,1,0:T(8,128)(2,1)} %bitcast.5), calls=%async_computation | async-start | bytes 2097152 | tf_op jit(solution)/shard_map/all_to_all | solution.py:134
  174.4 14.3 %copy-start.3 = (f32[512]{0:T(512)S(1)}, f32[512]{0:T(512)}, u32[]{:S(2)}) copy-start(f32[512]{0:T(512)} %param.15) | copy-start | bytes 6148
  176.2 12.5 %all-to-all-start.1 = ((f32[8,1,128]{2,1,0:T(1,128)}), f32[8,1,128]{2,1,0:T(1,128)S(1)}, u32[]{:S(2)}, u32[]{:S(2)}) async-start(f32[8,1,128]{2,1,0:T(1,128)} %broadcast_in_dim.43), calls=%async_computation.1 | async-start | bytes 8192 | tf_op jit(solution)/shard_map/all_to_all | solution.py:18
Sparse Core Ops, SparseCore 0:
  10.1 115.5 all-gather.2

commit v2 on v1

v2 whole, which is shorter than its diff:
```python
import functools
import math

import jax
import jax.numpy as jnp
from jax import lax
from jax.experimental import pallas as pl
from jax.experimental.pallas import tpu as pltpu
from jax.sharding import PartitionSpec as P

HEAD_WIDTH = 128
EXP_SCALE = HEAD_WIDTH ** (-0.5) * math.log2(math.e)
VMEM = pl.BlockSpec(memory_space=pltpu.VMEM)


def swapped(value):
    return lax.ppermute(value, "sub", [(0, 1), (1, 0)])


def attend_kernel(q_ref, k_ref, v_ref, kv_ref, pos_ref, limit_ref, out_ref, bias_ref):
    own, rows = k_ref.shape[0], q_ref.shape[0]
    keys = own // 4

    @pl.when(pl.program_id(0) == 0)
    def _():
        bias_ref[...] = jnp.where(pos_ref[...] < limit_ref[...], 0.0, -1e30)

    q = jnp.concatenate([q_ref[:, :HEAD_WIDTH], q_ref[:, HEAD_WIDTH:]], axis=0)
    scores = []
    for j in range(8):
        ref, at = (k_ref, j * keys) if j < 4 else (kv_ref, (j - 4) * keys)
        part = lax.dot_general(
            q, ref[at : at + keys], (((1,), (1,)), ((), ())), preferred_element_type=jnp.float32
        )
        bias = bias_ref[:, j * keys : (j + 1) * keys]
        scores.append(jnp.concatenate([part[:rows] + bias, part[rows:] + bias], axis=0))
    row_max = scores[0]
    for part in scores[1:]:
        row_max = jnp.maximum(row_max, part)
    row_max = jnp.max(row_max, axis=-1, keepdims=True) * EXP_SCALE
    total, product = 0.0, 0.0
    for j in range(8):
        ref, at = (v_ref, j * keys) if j < 4 else (kv_ref, own + (j - 4) * keys)
        weights = jnp.exp2(scores[j] * EXP_SCALE - row_max)
        total += weights
        product += jnp.dot(
            weights.astype(jnp.bfloat16), ref[at : at + keys], preferred_element_type=jnp.float32
        )
    result = (product / jnp.sum(total, axis=-1, keepdims=True)).astype(out_ref.dtype)
    out_ref[:, :HEAD_WIDTH] = result[:rows]
    out_ref[:, HEAD_WIDTH:] = result[rows:]


def attend(queries, keys, values, kv_other, key_pos, limit):
    rows, width = queries.shape
    heads, count = width // HEAD_WIDTH, key_pos.shape[1]
    whole = lambda a: pl.BlockSpec(a.shape, lambda h: (0, 0))
    return pl.pallas_call(
        attend_kernel,
        grid=(heads // 2,),
        in_specs=[
            pl.BlockSpec((rows, 2 * HEAD_WIDTH), lambda h: (0, h)),
            whole(keys),
            whole(values),
            whole(kv_other),
            whole(key_pos),
            whole(limit),
        ],
        out_specs=pl.BlockSpec((rows, 2 * HEAD_WIDTH), lambda h: (0, h)),
        out_shape=jax.ShapeDtypeStruct((rows, width), jnp.bfloat16),
        scratch_shapes=[pltpu.VMEM((rows, count), jnp.float32)],
        compiler_params=pltpu.CompilerParams(vmem_limit_bytes=32 << 20),
        cost_estimate=pl.CostEstimate(
            flops=4 * rows * width * count,
            bytes_accessed=4 * rows * width + 4 * count * HEAD_WIDTH,
            transcendentals=rows * heads * count,
        ),
    )(queries, keys, values, kv_other, key_pos, limit)


def project_kernel(a_ref, w_ref, out_ref):
    rows = out_ref.shape[2]
    block = jnp.concatenate([w_ref[j] for j in range(w_ref.shape[0])], axis=1)
    part = jnp.dot(a_ref[...], block, preferred_element_type=jnp.float32).astype(jnp.bfloat16)
    for c in range(out_ref.shape[1]):
        out_ref[0, c] = part[c * rows : (c + 1) * rows]


def project(both, weights, nx):
    chips, depth, wide = weights.shape
    rows, per = both.shape[0] // 2, chips // nx
    return pl.pallas_call(
        project_kernel,
        grid=(nx,),
        in_specs=[
            pl.BlockSpec(both.shape, lambda h: (0, 0)),
            pl.BlockSpec((per, depth, wide), lambda h: (h, 0, 0)),
        ],
        out_specs=pl.BlockSpec((1, 2, rows, per * wide), lambda h: (h, 0, 0, 0)),
        out_shape=jax.ShapeDtypeStruct((nx, 2, rows, per * wide), jnp.bfloat16),
        compiler_params=pltpu.CompilerParams(vmem_limit_bytes=121 << 19),
        cost_estimate=pl.CostEstimate(
            flops=4 * rows * depth * wide * chips,
            bytes_accessed=2 * weights.size,
            transcendentals=0,
        ),
    )(both, weights)


def add_kernel(parts_ref, residual_ref, hidden_ref, square_ref):
    shares, rows, columns = parts_ref.shape
    per = columns // HEAD_WIDTH
    squares = []
    for j in range(per):
        for c in range(2):
            span = slice((2 * j + c) * HEAD_WIDTH, (2 * j + c + 1) * HEAD_WIDTH)
            total = parts_ref[c, :, j * HEAD_WIDTH : (j + 1) * HEAD_WIDTH].astype(jnp.float32)
            for s in range(2 + c, shares, 2):
                total += parts_ref[s, :, j * HEAD_WIDTH : (j + 1) * HEAD_WIDTH].astype(jnp.float32)
            hidden = (residual_ref[:, span].astype(jnp.float32) + total).astype(jnp.bfloat16)
            hidden_ref[:, span] = hidden
            wide = hidden.astype(jnp.float32)
            squares.append(wide * wide)
    copies = square_ref.shape[0]
    square_ref[...] = lax.dot_general(
        jnp.ones((copies, HEAD_WIDTH), jnp.float32),
        sum(squares),
        (((1,), (1,)), ((), ())),
        precision=lax.Precision.HIGHEST,
        preferred_element_type=jnp.float32,
    )


def add_residual(parts, residual, nx):
    shape = residual.shape
    return pl.pallas_call(
        add_kernel,
        in_specs=[VMEM, VMEM],
        out_specs=(VMEM, VMEM),
        out_shape=(
            jax.ShapeDtypeStruct(shape, jnp.bfloat16),
            jax.ShapeDtypeStruct((nx, shape[0]), jnp.float32),
        ),
        compiler_params=pltpu.CompilerParams(vmem_limit_bytes=8 << 20),
        cost_estimate=pl.CostEstimate(
            flops=2 * parts.size, bytes_accessed=2 * parts.size, transcendentals=0
        ),
    )(parts, residual)


def norm_kernel(features, square_ref, hidden_ref, gain_ref, out_ref):
    total = lax.dot_general(
        square_ref[...],
        jnp.ones((square_ref.shape[0], HEAD_WIDTH), jnp.float32),
        (((0,), (0,)), ((), ())),
        precision=lax.Precision.HIGHEST,
        preferred_element_type=jnp.float32,
    )
    factor = lax.rsqrt(total / features + 1e-06)
    for at in range(0, hidden_ref.shape[1], HEAD_WIDTH):
        span = slice(at, at + HEAD_WIDTH)
        wide = hidden_ref[:, span].astype(jnp.float32)
        out_ref[:, span] = (wide * factor * gain_ref[:, span]).astype(jnp.bfloat16)


def normalise(squares, hidden, gain, features):
    return pl.pallas_call(
        functools.partial(norm_kernel, features),
        in_specs=[VMEM, VMEM, VMEM],
        out_specs=VMEM,
        out_shape=jax.ShapeDtypeStruct(hidden.shape, jnp.bfloat16),
        compiler_params=pltpu.CompilerParams(vmem_limit_bytes=8 << 20),
        cost_estimate=pl.CostEstimate(
            flops=4 * hidden.size, bytes_accessed=4 * hidden.size, transcendentals=0
        ),
    )(squares, hidden, gain[None, :])


def shards(queries, keys, values, half_order, frame_lengths, out_proj, residual_in, norm_gain):
    tok_rows = queries.shape[0]
    half_rows = tok_rows // 2
    chips, nx = lax.axis_size("seq"), lax.axis_size("heads")
    z, core = lax.axis_index("seq"), lax.axis_index("sub")
    features = residual_in.shape[1] * nx

    weights = lax.all_gather(out_proj, "seq")
    k_own = lax.all_gather(keys, "seq", tiled=True)
    v_own = lax.all_gather(values, "seq", tiled=True)
    kv_other = swapped(jnp.concatenate([k_own, v_own], axis=0))

    inner = jnp.arange(half_rows, dtype=jnp.int32)
    table = (half_order[:, None] * half_rows + inner[None, :]).reshape(chips, 2, tok_rows)
    of_core = [table[:, 0].reshape(1, -1), table[:, 1].reshape(1, -1)]
    key_pos = jnp.where(
        core == 0,
        jnp.concatenate(of_core, axis=1),
        jnp.concatenate(of_core[::-1], axis=1),
    )
    chosen = (jnp.arange(2 * chips, dtype=jnp.int32) == 2 * z + core)[:, None]
    query_pos = jnp.sum(jnp.where(chosen, table.reshape(2 * chips, tok_rows), 0), axis=0)
    frame_starts = jnp.cumsum(frame_lengths) - frame_lengths
    limit = jnp.sum(
        jnp.where(frame_starts[None, :] <= query_pos[:, None], frame_lengths[None, :], 0), axis=1
    )[:, None]
    attended = attend(queries, k_own, v_own, kv_other, key_pos, limit)

    both = lax.all_gather(attended, "sub", tiled=True)
    parts = project(both, weights, nx).reshape(2 * nx, tok_rows, -1)
    parts = lax.all_to_all(parts, ("heads", "sub"), 0, 0, tiled=True)
    hidden_state, squares = add_residual(parts, residual_in, nx)
    squares = lax.all_to_all(squares, "heads", 0, 0, tiled=True)
    normed = normalise(squares, hidden_state, norm_gain, features)
    return (attended, hidden_state, normed)


def solution(mesh):
    rows = P(("groups", "seq", "sub"), "heads")
    in_specs = (rows, rows, rows, P("groups"), P("groups"), P("heads", ("seq", "sub")), rows, P("heads"))
    return jax.shard_map(
        shards, mesh=mesh, in_specs=in_specs, out_specs=(rows, rows, rows), check_vma=False
    )
```

time: 197 us -> 196 us (level)
  blocking collectives: 109 us -> 157 us
  waiting for transfers between devices: 35 us -> 2 us
  starting transfers between devices: 14.5 us -> 2.01 us
  local copies, waits for them, and re-layouts: 6.49 us -> 1.77 us
  Pallas kernels: 15.6 us -> 18.3 us
    all_to_all x0 -> x2, blocking collectives: none -> 46.3 us  [the longest x1 34.6 us: shards(): parts = lax.all_to_all(parts, ('heads', 'sub'), 0, 0, tiled=True)]
    all_to_all x2 -> x0, waiting for transfers between devices: 33 us -> none  [the longest x1 26.2 us: shards(): parts = lax.all_to_all(parts, ('heads', 'sub'), 0, 0, tiled=True)]
    all_to_all x2 -> x0, starting transfers between devices: 12.5 us -> none  [the longest x1 7.67 us: shards(): parts = lax.all_to_all(parts, ('heads', 'sub'), 0, 0, tiled=True)]
    unnamed x15 -> x12, local copies, waits for them, and re-layouts: 3.87 us -> 0.92 us
    pallas_call x1, Pallas kernels: 4.76 us -> 7.1 us  [project(): pl.pallas_call(project_kernel, grid=(nx,), in_specs=[pl.BlockSpec(both.sh...]
    pallas_call x1 -> x3, Pallas kernels: 10.8 us -> 11.2 us  [the longest x1 9.46 us: attend(): pl.pallas_call(attend_kernel, grid=(heads // 2,), in_specs=[pl.BlockSpec(...]
  transfers between devices with their start and end apart: 4 -> 2, of which waited for: 3 -> 1; matrix products, arithmetic and copies ran while one was open for 1% -> 1% of each run, Pallas kernels for 5% -> 5%
where the time goes in v2:
time: 196 us; the launch traced here: 195 us
  blocking collectives  157 us (80%)
  Pallas kernels  18.3 us (9%)
  between operations  14.2 us (7%)
  starting transfers between devices  2.01 us (1%)
  waiting for transfers between devices  2 us (1%)
    all_gather x1, blocking collectives, shards(): k_own = lax.all_gather(keys, 'seq', tiled=True)  72.3 us
    all_to_all x1, blocking collectives, shards(): parts = lax.all_to_all(parts, ('heads', 'sub'), 0, 0, tiled=True)  34.6 us
    all_gather x1, blocking collectives, shards(): v_own = lax.all_gather(values, 'seq', tiled=True)  34.2 us
    all_to_all x1, blocking collectives, shards(): squares = lax.all_to_all(squares, 'heads', 0, 0, tiled=True)  11.6 us
    pallas_call x1, Pallas kernels, attend(): pl.pallas_call(attend_kernel, grid=(heads // 2,), in_specs=[pl.BlockSpec(...  9.46 us
    pallas_call x1, Pallas kernels, project(): pl.pallas_call(project_kernel, grid=(nx,), in_specs=[pl.BlockSpec(both.sh...  7.1 us
  transfers between devices with their start and end apart: 2, of which 1 were waited for; matrix products, arithmetic and copies ran while one was open for 1% of the time, Pallas kernels for 5%

profile of v2, /device:TPU:80, one launch (start us, length us, event | category | flops | bytes accessed | tf_op | source)
XLA Modules:
  0.0 195.5 jit_solution(18053220341938879203)
XLA Ops:
  7.2 0.0 copy-start.5
  7.2 0.0 copy-start.4
  7.2 0.0 copy-start.3
  7.2 0.1 all-gather.3.cloned.1.call-start
  7.3 0.7 all-gather.3.cloned.1.call-update
  8.0 72.3 %all_gather.15.k_ref = bf16[2048,128]{1,0:T(8,128)(2,1)S(1)} all-gather(bf16[128,128]{1,0:T(8,128)(2,1)} %param.9), channel_id=1, replica_groups=mesh['groups'=2,'seq'=16,'heads'=8,'sub'=2] {'seq'}, dimensions={0}, use_global_device_ids=true | all-gather | bytes 557056 | tf_op jit(solution)/shard_map/all_gather | solution.py:187
  80.3 34.2 %all_gather.16.v_ref = bf16[2048,128]{1,0:T(8,128)(2,1)S(1)} all-gather(bf16[128,128]{1,0:T(8,128)(2,1)} %param.10), channel_id=1, replica_groups=mesh['groups'=2,'seq'=16,'heads'=8,'sub'=2] {'seq'}, dimensions={0}, use_global_device_ids=true | all-gather | bytes 557056 | tf_op jit(solution)/shard_map/all_gather | solution.py:188
  114.6 0.1 pad_maximum_fusion
  114.6 2.0 collective-permute-start
  116.6 0.0 copy-done.5
  116.6 0.1 add.43
  116.7 0.1 copy.23
  116.8 0.1 select_reduce_fusion
  116.9 0.1 add.35
  117.1 0.1 add.36
  117.1 0.1 add.37
  117.2 0.1 add.39
  117.3 0.1 le.16
  117.4 0.1 copy.22
  117.5 0.1 reduce-window.9
  117.6 0.1 reduce.1
  117.7 0.1 select_reduce_fusion.1
  117.8 0.1 copy.24.limit_ref
  117.9 1.3 collective-permute-done.kv_ref
  119.2 9.5 %shard_map.103 = bf16[128,1024]{1,0:T(8,128)(2,1)} custom-call(bf16[128,1024]{1,0:T(8,128)(2,1)S(1)} %copy-done.3, bf16[2048,128]{1,0:T(8,128)(2,1)S(1)} %all_gather.15.k_ref, bf16[2048,128]{1,0:T(8,128)(2,1)S(1)} %all_gather.16.v_ref, bf16[4096,128]{1,0:T(8,128)(2,1)S(1)} %collective-permute-done.kv_ref, s32[1,4096]{1,0:T(1,128)S(1)} %broadcast_select_fusion.pos_ref, ...), custom_call_target="tpu_custom_call" | custom-call | flops 2147483648 | bytes 2621440 | tf_op jit(solution)/shard_map/pallas_call | solution.py:58
  128.7 3.9 %all_gather.17.a_ref = bf16[256,1024]{1,0:T(8,128)(2,1)} all-gather(bf16[128,1024]{1,0:T(8,128)(2,1)} %shard_map.103), channel_id=1, replica_groups=mesh['groups'=2,'seq'=16,'heads'=8,'sub'=2] {'sub'}, dimensions={0}, use_global_device_ids=true | all-gather | bytes 786432 | tf_op jit(solution)/shard_map/all_gather | solution.py:207
  132.6 7.1 %shard_map.104 = bf16[8,2,128,256]{3,2,1,0:T(8,128)(2,1)} custom-call(bf16[256,1024]{1,0:T(8,128)(2,1)} %all_gather.17.a_ref, bf16[16,1024,128]{2,1,0:T(8,128)(2,1)} %bitcast.16), custom_call_target="tpu_custom_call" | custom-call | flops 1073741824 | bytes 4194304 | tf_op jit(solution)/shard_map/pallas_call | solution.py:92
  139.7 34.6 %all_to_all.16.parts_ref = bf16[16,128,256]{2,1,0:T(8,128)(2,1)S(1)} all-to-all(bf16[16,128,256]{2,1,0:T(8,128)(2,1)} %bitcast.17), channel_id=1, replica_groups=mesh['groups'=2,'seq'=16,'heads'=8,'sub'=2] {'heads','sub'}, dimensions={0} | all-to-all | bytes 2097152 | tf_op jit(solution)/shard_map/all_to_all | solution.py:209
  174.3 0.8 shard_map.105
  175.1 11.6 %all_to_all.17 = f32[8,1,128]{2,1,0:T(1,128)S(1)} all-to-all(f32[8,1,128]{2,1,0:T(1,128)S(1)} %bitcast.14), channel_id=1, replica_groups=mesh['groups'=2,'seq'=16,'heads'=8,'sub'=2] {'heads'}, dimensions={0} | all-to-all | bytes 8192 | tf_op jit(solution)/shard_map/all_to_all | solution.py:211
  186.8 0.9 copy-done.1
  187.7 0.9 shard_map.106
  (16 shorter events, 0.1 us)
Async XLA Ops:
  7.2 109.4 %copy-start.5 = (s32[64]{0:T(128)S(1)}, s32[64]{0:T(128)}, u32[]{:S(2)}) copy-start(s32[64]{0:T(128)} %param.11) | copy-start | bytes 772
  7.2 110.2 %copy-start.4 = (s32[32]{0:T(128)S(1)}, s32[32]{0:T(128)}, u32[]{:S(2)}) copy-start(s32[32]{0:T(128)} %param.12) | copy-start | bytes 388
  7.2 112.0 %copy-start.3 = (bf16[128,1024]{1,0:T(8,128)(2,1)S(1)}, bf16[128,1024]{1,0:T(8,128)(2,1)}, u32[]{:S(2)}) copy-start(bf16[128,1024]{1,0:T(8,128)(2,1)} %q_ref.1) | copy-start | bytes 786436
  7.2 125.3 %all-gather.3.cloned.1.call-start = ((), (), s32[]{:S(2)}) async-start(), calls=%async_computation.2 | async-start | bytes 4456448 | tf_op jit(solution)/shard_map/all_gather | solution.py:186
  114.6 4.6 %collective-permute-start = (bf16[4096,128]{1,0:T(8,128)(2,1)S(1)}, bf16[4096,128]{1,0:T(8,128)(2,1)S(1)}, u32[]{:S(2)}, u32[]{:S(2)}) collective-permute-start(bf16[4096,128]{1,0:T(8,128)(2,1)S(1)} %pad_maximum_fusion), channel_id=1, source_target_pairs={{0,1},{1,0},{2,3},{3,2},{4,5},{5,4},{6,7},{7,6},{8,9},{9,8},{10,11... | collective-permute-start | bytes 3145736 | tf_op jit(solution)/shard_map/ppermute | solution.py:17
  139.7 34.6 %copy-start = (bf16[128,512]{1,0:T(8,128)(2,1)S(1)}, bf16[128,512]{1,0:T(8,128)(2,1)}, u32[]{:S(2)}) copy-start(bf16[128,512]{1,0:T(8,128)(2,1)} %residual_ref.1) | copy-start | bytes 393220
  139.7 47.1 %copy-start.2 = (f32[512]{0:T(512)S(1)}, f32[512]{0:T(512)}, u32[]{:S(2)}) copy-start(f32[512]{0:T(512)} %param.15) | copy-start | bytes 6148
  186.8 0.9 copy-start.1
Sparse Core Ops, SparseCore 0:
  10.1 115.5 all-gather.2

commit v3 on v2

--- a/solution.py
+++ b/solution.py
@@ -10,6 +10,7 @@
 
 HEAD_WIDTH = 128
 EXP_SCALE = HEAD_WIDTH ** (-0.5) * math.log2(math.e)
+STRETCHES, STEP_HEADS = 8, 4
 VMEM = pl.BlockSpec(memory_space=pltpu.VMEM)
 
 
@@ -19,54 +20,71 @@
 
 def attend_kernel(q_ref, k_ref, v_ref, kv_ref, pos_ref, limit_ref, out_ref, bias_ref):
     own, rows = k_ref.shape[0], q_ref.shape[0]
-    keys = own // 4
+    heads, half = q_ref.shape[1] // HEAD_WIDTH, STRETCHES // 2
+    keys = own // half
 
     @pl.when(pl.program_id(0) == 0)
     def _():
         bias_ref[...] = jnp.where(pos_ref[...] < limit_ref[...], 0.0, -1e30)
 
-    q = jnp.concatenate([q_ref[:, :HEAD_WIDTH], q_ref[:, HEAD_WIDTH:]], axis=0)
-    scores = []
-    for j in range(8):
-        ref, at = (k_ref, j * keys) if j < 4 else (kv_ref, (j - 4) * keys)
-        part = lax.dot_general(
+    spans = [slice(i * HEAD_WIDTH, (i + 1) * HEAD_WIDTH) for i in range(heads)]
+    parts = [slice(i * rows, (i + 1) * rows) for i in range(heads)]
+    q = jnp.concatenate([q_ref[:, span] for span in spans], axis=0)
+
+    def scored(j):
+        ref, at = (k_ref, j * keys) if j < half else (kv_ref, (j - half) * keys)
+        product = lax.dot_general(
             q, ref[at : at + keys], (((1,), (1,)), ((), ())), preferred_element_type=jnp.float32
         )
         bias = bias_ref[:, j * keys : (j + 1) * keys]
-        scores.append(jnp.concatenate([part[:rows] + bias, part[rows:] + bias], axis=0))
-    row_max = scores[0]
-    for part in scores[1:]:
-        row_max = jnp.maximum(row_max, part)
-    row_max = jnp.max(row_max, axis=-1, keepdims=True) * EXP_SCALE
-    total, product = 0.0, 0.0
-    for j in range(8):
-        ref, at = (v_ref, j * keys) if j < 4 else (kv_ref, own + (j - 4) * keys)
-        weights = jnp.exp2(scores[j] * EXP_SCALE - row_max)
-        total += weights
-        product += jnp.dot(
-            weights.astype(jnp.bfloat16), ref[at : at + keys], preferred_element_type=jnp.float32
+        return [product[part] + bias for part in parts]
+
+    scores = scored(0)
+    top, total, result = [None] * heads, [None] * heads, [None] * heads
+    for j in range(STRETCHES):
+        coming = scored(j + 1) if j + 1 < STRETCHES else None
+        ref, at = (v_ref, j * keys) if j < half else (kv_ref, own + (j - half) * keys)
+        weights, fades = [], []
+        for i in range(heads):
+            peak = jnp.max(scores[i], axis=-1, keepdims=True) * EXP_SCALE
+            if j:
+                peak = jnp.maximum(peak, top[i])
+            weight = jnp.exp2(scores[i] * EXP_SCALE - peak)
+            mass = jnp.sum(weight, axis=-1, keepdims=True)
+            if j:
+                fades.append(jnp.exp2(top[i] - peak))
+                mass += total[i] * fades[i]
+            top[i], total[i] = peak, mass
+            weights.append(weight.astype(jnp.bfloat16))
+        product = jnp.dot(
+            jnp.concatenate(weights, axis=0),
+            ref[at : at + keys],
+            preferred_element_type=jnp.float32,
         )
-    result = (product / jnp.sum(total, axis=-1, keepdims=True)).astype(out_ref.dtype)
-    out_ref[:, :HEAD_WIDTH] = result[:rows]
-    out_ref[:, HEAD_WIDTH:] = result[rows:]
+        for i in range(heads):
+            result[i] = product[parts[i]] + (result[i] * fades[i] if j else 0.0)
+        scores = coming
+    for i in range(heads):
+        out_ref[:, spans[i]] = (result[i] / total[i]).astype(out_ref.dtype)
 
 
 def attend(queries, keys, values, kv_other, key_pos, limit):
     rows, width = queries.shape
     heads, count = width // HEAD_WIDTH, key_pos.shape[1]
+    wide = STEP_HEADS * HEAD_WIDTH
     whole = lambda a: pl.BlockSpec(a.shape, lambda h: (0, 0))
     return pl.pallas_call(
         attend_kernel,
-        grid=(heads // 2,),
+        grid=(width // wide,),
         in_specs=[
-            pl.BlockSpec((rows, 2 * HEAD_WIDTH), lambda h: (0, h)),
+            pl.BlockSpec((rows, wide), lambda h: (0, h)),
             whole(keys),
             whole(values),
             whole(kv_other),
             whole(key_pos),
             whole(limit),
         ],
-        out_specs=pl.BlockSpec((rows, 2 * HEAD_WIDTH), lambda h: (0, h)),
+        out_specs=pl.BlockSpec((rows, wide), lambda h: (0, h)),
         out_shape=jax.ShapeDtypeStruct((rows, width), jnp.bfloat16),
         scratch_shapes=[pltpu.VMEM((rows, count), jnp.float32)],
         compiler_params=pltpu.CompilerParams(vmem_limit_bytes=32 << 20),
@@ -80,25 +98,27 @@
 
 def project_kernel(a_ref, w_ref, out_ref):
     rows = out_ref.shape[2]
-    block = jnp.concatenate([w_ref[j] for j in range(w_ref.shape[0])], axis=1)
-    part = jnp.dot(a_ref[...], block, preferred_element_type=jnp.float32).astype(jnp.bfloat16)
-    for c in range(out_ref.shape[1]):
-        out_ref[0, c] = part[c * rows : (c + 1) * rows]
+    per = w_ref.shape[0] // out_ref.shape[0]
+    for h in range(out_ref.shape[0]):
+        block = jnp.concatenate([w_ref[per * h + j] for j in range(per)], axis=1)
+        part = jnp.dot(a_ref[...], block, preferred_element_type=jnp.float32).astype(jnp.bfloat16)
+        for c in range(2):
+            out_ref[h, c] = part[c * rows : (c + 1) * rows]
 
 
 def project(both, weights, nx):
     chips, depth, wide = weights.shape
-    rows, per = both.shape[0] // 2, chips // nx
+    rows, per, steps = both.shape[0] // 2, chips // nx, 2
     return pl.pallas_call(
         project_kernel,
-        grid=(nx,),
+        grid=(steps,),
         in_specs=[
             pl.BlockSpec(both.shape, lambda h: (0, 0)),
-            pl.BlockSpec((per, depth, wide), lambda h: (h, 0, 0)),
+            pl.BlockSpec((chips // steps, depth, wide), lambda h: (h, 0, 0)),
         ],
-        out_specs=pl.BlockSpec((1, 2, rows, per * wide), lambda h: (h, 0, 0, 0)),
+        out_specs=pl.BlockSpec((nx // steps, 2, rows, per * wide), lambda h: (h, 0, 0, 0)),
         out_shape=jax.ShapeDtypeStruct((nx, 2, rows, per * wide), jnp.bfloat16),
-        compiler_params=pltpu.CompilerParams(vmem_limit_bytes=121 << 19),
+        compiler_params=pltpu.CompilerParams(vmem_limit_bytes=52 << 20),
         cost_estimate=pl.CostEstimate(
             flops=4 * rows * depth * wide * chips,
             bytes_accessed=2 * weights.size,
@@ -109,14 +129,14 @@
 
 def add_kernel(parts_ref, residual_ref, hidden_ref, square_ref):
     shares, rows, columns = parts_ref.shape
-    per = columns // HEAD_WIDTH
     squares = []
-    for j in range(per):
+    for j in range(columns // HEAD_WIDTH):
+        at = slice(j * HEAD_WIDTH, (j + 1) * HEAD_WIDTH)
         for c in range(2):
             span = slice((2 * j + c) * HEAD_WIDTH, (2 * j + c + 1) * HEAD_WIDTH)
-            total = parts_ref[c, :, j * HEAD_WIDTH : (j + 1) * HEAD_WIDTH].astype(jnp.float32)
+            total = parts_ref[c, :, at].astype(jnp.float32)
             for s in range(2 + c, shares, 2):
-                total += parts_ref[s, :, j * HEAD_WIDTH : (j + 1) * HEAD_WIDTH].astype(jnp.float32)
+                total += parts_ref[s, :, at].astype(jnp.float32)
             hidden = (residual_ref[:, span].astype(jnp.float32) + total).astype(jnp.bfloat16)
             hidden_ref[:, span] = hidden
             wide = hidden.astype(jnp.float32)

time: 196 us -> 188 us (0.959)
  Pallas kernels: 18.3 us -> 12.1 us
  blocking collectives: 157 us -> 155 us
    pallas_call x2, Pallas kernels: 16.6 us -> 10.3 us  [the longest x1 7.24 us: attend(): pl.pallas_call(attend_kernel, grid=(width // wide,), in_specs=[pl.BlockSp...]
  transfers between devices with their start and end apart: 2 -> 2, of which waited for: 1 -> 1; matrix products, arithmetic and copies ran while one was open for 1% -> 1% of each run, Pallas kernels for 5% -> 4%
where the time goes in v3:
time: 188 us
  blocking collectives  155 us (82%)
  between operations  14.2 us (8%)
  Pallas kernels  12.1 us (6%)
  starting transfers between devices  2.01 us (1%)
  waiting for transfers between devices  2 us (1%)
    all_gather x1, blocking collectives, shards(): k_own = lax.all_gather(keys, 'seq', tiled=True)  72.3 us
    all_to_all x1, blocking collectives, shards(): parts = lax.all_to_all(parts, ('heads', 'sub'), 0, 0, tiled=True)  34.4 us
    all_gather x1, blocking collectives, shards(): v_own = lax.all_gather(values, 'seq', tiled=True)  34.2 us
    all_to_all x1, blocking collectives, shards(): squares = lax.all_to_all(squares, 'heads', 0, 0, tiled=True)  11.6 us
    pallas_call x1, Pallas kernels, attend(): pl.pallas_call(attend_kernel, grid=(width // wide,), in_specs=[pl.BlockSp...  7.24 us
  transfers between devices with their start and end apart: 2, of which 1 were waited for; matrix products, arithmetic and copies ran while one was open for 1% of the time, Pallas kernels for 4%

profile of v3, /device:TPU:80, one launch (start us, length us, event | category | flops | bytes accessed | tf_op | source)
XLA Modules:
  0.0 187.6 jit_solution(9292840543511799421)
XLA Ops:
  7.2 0.1 all-gather.3.cloned.1.call-start
  7.3 0.7 all-gather.3.cloned.1.call-update
  8.0 72.3 %all_gather.15.k_ref = bf16[2048,128]{1,0:T(8,128)(2,1)S(1)} all-gather(bf16[128,128]{1,0:T(8,128)(2,1)} %param.9), channel_id=1, replica_groups=mesh['groups'=2,'seq'=16,'heads'=8,'sub'=2] {'seq'}, dimensions={0}, use_global_device_ids=true | all-gather | bytes 557056 | tf_op jit(solution)/shard_map/all_gather | solution.py:207
  80.3 34.2 %all_gather.16.v_ref = bf16[2048,128]{1,0:T(8,128)(2,1)S(1)} all-gather(bf16[128,128]{1,0:T(8,128)(2,1)} %param.10), channel_id=1, replica_groups=mesh['groups'=2,'seq'=16,'heads'=8,'sub'=2] {'seq'}, dimensions={0}, use_global_device_ids=true | all-gather | bytes 557056 | tf_op jit(solution)/shard_map/all_gather | solution.py:208
  114.6 0.1 pad_maximum_fusion
  114.6 2.0 %collective-permute-start = (bf16[4096,128]{1,0:T(8,128)(2,1)S(1)}, bf16[4096,128]{1,0:T(8,128)(2,1)S(1)}, u32[]{:S(2)}, u32[]{:S(2)}) collective-permute-start(bf16[4096,128]{1,0:T(8,128)(2,1)S(1)} %pad_maximum_fusion), channel_id=1, source_target_pairs={{0,1},{1,0},{2,3},{3,2},{4,5},{5,4},{6,7},{7,6},{8,9},{9,8},{10,11... | collective-permute-start | bytes 3145736 | tf_op jit(solution)/shard_map/ppermute | solution.py:18
  116.6 0.1 add.43
  116.7 0.1 copy.23
  116.8 0.1 select_reduce_fusion
  116.9 0.1 add.35
  117.1 0.1 add.36
  117.1 0.1 add.37
  117.2 0.1 add.39
  117.3 0.1 le.16
  117.4 0.1 copy.22
  117.5 0.1 reduce-window.9
  117.6 0.1 reduce.1
  117.7 0.1 select_reduce_fusion.1
  117.8 0.1 copy.24.limit_ref
  117.9 1.3 collective-permute-done.kv_ref
  119.2 0.0 copy-done.3
  119.2 7.2 %shard_map.103 = bf16[128,1024]{1,0:T(8,128)(2,1)} custom-call(bf16[128,1024]{1,0:T(8,128)(2,1)S(1)} %copy-done.3, bf16[2048,128]{1,0:T(8,128)(2,1)S(1)} %all_gather.15.k_ref, bf16[2048,128]{1,0:T(8,128)(2,1)S(1)} %all_gather.16.v_ref, bf16[4096,128]{1,0:T(8,128)(2,1)S(1)} %collective-permute-done.kv_ref, s32[1,4096]{1,0:T(1,128)S(1)} %broadcast_select_fusion.pos_ref, ...), custom_call_target="tpu_custom_call" | custom-call | flops 2147483648 | bytes 2621440 | tf_op jit(solution)/shard_map/pallas_call | solution.py:76
  126.5 2.4 %all_gather.17.a_ref = bf16[256,1024]{1,0:T(8,128)(2,1)S(1)} all-gather(bf16[128,1024]{1,0:T(8,128)(2,1)} %shard_map.103), channel_id=1, replica_groups=mesh['groups'=2,'seq'=16,'heads'=8,'sub'=2] {'sub'}, dimensions={0}, use_global_device_ids=true | all-gather | bytes 786432 | tf_op jit(solution)/shard_map/all_gather | solution.py:227
  128.9 3.0 %shard_map.104 = bf16[8,2,128,256]{3,2,1,0:T(8,128)(2,1)S(1)} custom-call(bf16[256,1024]{1,0:T(8,128)(2,1)S(1)} %all_gather.17.a_ref, bf16[16,1024,128]{2,1,0:T(8,128)(2,1)} %bitcast.17), custom_call_target="tpu_custom_call" | custom-call | flops 1073741824 | bytes 4194304 | tf_op jit(solution)/shard_map/pallas_call | solution.py:112
  131.9 0.0 copy-start
  131.9 0.0 copy-start.2
  132.0 34.4 %all_to_all.16.parts_ref = bf16[16,128,256]{2,1,0:T(8,128)(2,1)S(1)} all-to-all(bf16[16,128,256]{2,1,0:T(8,128)(2,1)S(1)} %bitcast.13), channel_id=1, replica_groups=mesh['groups'=2,'seq'=16,'heads'=8,'sub'=2] {'heads','sub'}, dimensions={0} | all-to-all | bytes 2097152 | tf_op jit(solution)/shard_map/all_to_all | solution.py:229
  166.4 0.0 copy-done
  166.4 0.8 shard_map.105
  167.2 11.6 %all_to_all.17 = f32[8,1,128]{2,1,0:T(1,128)S(1)} all-to-all(f32[8,1,128]{2,1,0:T(1,128)S(1)} %bitcast.15), channel_id=1, replica_groups=mesh['groups'=2,'seq'=16,'heads'=8,'sub'=2] {'heads'}, dimensions={0} | all-to-all | bytes 8192 | tf_op jit(solution)/shard_map/all_to_all | solution.py:231
  178.9 0.9 copy-done.1
  179.8 0.9 shard_map.106
  (16 shorter events, 0.1 us)
Async XLA Ops:
  7.2 109.4 %copy-start.5 = (s32[64]{0:T(128)S(1)}, s32[64]{0:T(128)}, u32[]{:S(2)}) copy-start(s32[64]{0:T(128)} %param.11) | copy-start | bytes 772
  7.2 110.2 %copy-start.4 = (s32[32]{0:T(128)S(1)}, s32[32]{0:T(128)}, u32[]{:S(2)}) copy-start(s32[32]{0:T(128)} %param.12) | copy-start | bytes 388
  7.2 112.0 %copy-start.3 = (bf16[128,1024]{1,0:T(8,128)(2,1)S(1)}, bf16[128,1024]{1,0:T(8,128)(2,1)}, u32[]{:S(2)}) copy-start(bf16[128,1024]{1,0:T(8,128)(2,1)} %q_ref.1) | copy-start | bytes 786436
  7.2 121.7 %all-gather.3.cloned.1.call-start = ((), (), s32[]{:S(2)}) async-start(), calls=%async_computation.2 | async-start | bytes 4456448 | tf_op jit(solution)/shard_map/all_gather | solution.py:206
  114.6 4.6 %collective-permute-start = (bf16[4096,128]{1,0:T(8,128)(2,1)S(1)}, bf16[4096,128]{1,0:T(8,128)(2,1)S(1)}, u32[]{:S(2)}, u32[]{:S(2)}) collective-permute-start(bf16[4096,128]{1,0:T(8,128)(2,1)S(1)} %pad_maximum_fusion), channel_id=1, source_target_pairs={{0,1},{1,0},{2,3},{3,2},{4,5},{5,4},{6,7},{7,6},{8,9},{9,8},{10,11... | collective-permute-start | bytes 3145736 | tf_op jit(solution)/shard_map/ppermute | solution.py:18
  131.9 34.5 %copy-start = (bf16[128,512]{1,0:T(8,128)(2,1)S(1)}, bf16[128,512]{1,0:T(8,128)(2,1)}, u32[]{:S(2)}) copy-start(bf16[128,512]{1,0:T(8,128)(2,1)} %residual_ref.1) | copy-start | bytes 393220
  131.9 46.9 %copy-start.2 = (f32[512]{0:T(512)S(1)}, f32[512]{0:T(512)}, u32[]{:S(2)}) copy-start(f32[512]{0:T(512)} %param.15) | copy-start | bytes 6148
  178.9 0.9 copy-start.1
Sparse Core Ops, SparseCore 0:
  10.1 115.5 all-gather.2

commit v4 on v3

--- a/solution.py
+++ b/solution.py
@@ -10,7 +10,7 @@
 
 HEAD_WIDTH = 128
 EXP_SCALE = HEAD_WIDTH ** (-0.5) * math.log2(math.e)
-STRETCHES, STEP_HEADS = 8, 4
+STRETCHES, STEP_HEADS = 4, 4
 VMEM = pl.BlockSpec(memory_space=pltpu.VMEM)
 
 
@@ -18,82 +18,88 @@
     return lax.ppermute(value, "sub", [(0, 1), (1, 0)])
 
 
-def attend_kernel(q_ref, k_ref, v_ref, kv_ref, pos_ref, limit_ref, out_ref, bias_ref):
-    own, rows = k_ref.shape[0], q_ref.shape[0]
-    heads, half = q_ref.shape[1] // HEAD_WIDTH, STRETCHES // 2
-    keys = own // half
-
-    @pl.when(pl.program_id(0) == 0)
-    def _():
-        bias_ref[...] = jnp.where(pos_ref[...] < limit_ref[...], 0.0, -1e30)
-
-    spans = [slice(i * HEAD_WIDTH, (i + 1) * HEAD_WIDTH) for i in range(heads)]
-    parts = [slice(i * rows, (i + 1) * rows) for i in range(heads)]
-    q = jnp.concatenate([q_ref[:, span] for span in spans], axis=0)
-
-    def scored(j):
-        ref, at = (k_ref, j * keys) if j < half else (kv_ref, (j - half) * keys)
-        product = lax.dot_general(
-            q, ref[at : at + keys], (((1,), (1,)), ((), ())), preferred_element_type=jnp.float32
-        )
-        bias = bias_ref[:, j * keys : (j + 1) * keys]
-        return [product[part] + bias for part in parts]
-
-    scores = scored(0)
-    top, total, result = [None] * heads, [None] * heads, [None] * heads
-    for j in range(STRETCHES):
-        coming = scored(j + 1) if j + 1 < STRETCHES else None
-        ref, at = (v_ref, j * keys) if j < half else (kv_ref, own + (j - half) * keys)
-        weights, fades = [], []
-        for i in range(heads):
-            peak = jnp.max(scores[i], axis=-1, keepdims=True) * EXP_SCALE
-            if j:
-                peak = jnp.maximum(peak, top[i])
-            weight = jnp.exp2(scores[i] * EXP_SCALE - peak)
-            mass = jnp.sum(weight, axis=-1, keepdims=True)
-            if j:
-                fades.append(jnp.exp2(top[i] - peak))
-                mass += total[i] * fades[i]
-            top[i], total[i] = peak, mass
-            weights.append(weight.astype(jnp.bfloat16))
-        product = jnp.dot(
-            jnp.concatenate(weights, axis=0),
-            ref[at : at + keys],
-            preferred_element_type=jnp.float32,
-        )
-        for i in range(heads):
-            result[i] = product[parts[i]] + (result[i] * fades[i] if j else 0.0)
-        scores = coming
-    for i in range(heads):
-        out_ref[:, spans[i]] = (result[i] / total[i]).astype(out_ref.dtype)
-
-
-def attend(queries, keys, values, kv_other, key_pos, limit):
+def attend_kernel(first, q_ref, k_ref, v_ref, pos_ref, limit_ref, *refs):
+    if first:
+        top_ref, total_ref, result_ref, bias_ref = refs
+    else:
+        top_in, total_in, result_in, out_ref, bias_ref = refs
+    rows, width = q_ref.shape
+    keys = k_ref.shape[0] // STRETCHES
+    bias_ref[...] = jnp.where(pos_ref[...] < limit_ref[...], 0.0, -1e30)
+    parts = [slice(i * rows, (i + 1) * rows) for i in range(STEP_HEADS)]
+
+    for group in range(0, width // HEAD_WIDTH, STEP_HEADS):
+        spans = [
+            slice(i * HEAD_WIDTH, (i + 1) * HEAD_WIDTH) for i in range(group, group + STEP_HEADS)
+        ]
+        q = jnp.concatenate([q_ref[:, span] for span in spans], axis=0)
+
+        def scored(j):
+            product = lax.dot_general(
+                q,
+                k_ref[j * keys : (j + 1) * keys],
+                (((1,), (1,)), ((), ())),
+                preferred_element_type=jnp.float32,
+            )
+            bias = bias_ref[:, j * keys : (j + 1) * keys]
+            return [product[part] + bias for part in parts]
+
+        scores = scored(0)
+        if first:
+            top, total, result = ([None] * STEP_HEADS for _ in range(3))
+        else:
+            top = [top_in[:, span][:, :1] for span in spans]
+            total = [total_in[:, span][:, :1] for span in spans]
+            result = [result_in[:, span] for span in spans]
+        for j in range(STRETCHES):
+            coming = scored(j + 1) if j + 1 < STRETCHES else None
+            fresh = first and j == 0
+            weights, fades = [], []
+            for i in range(STEP_HEADS):
+                peak = jnp.max(scores[i], axis=-1, keepdims=True) * EXP_SCALE
+                if not fresh:
+                    peak = jnp.maximum(peak, top[i])
+                weight = jnp.exp2(scores[i] * EXP_SCALE - peak)
+                mass = jnp.sum(weight, axis=-1, keepdims=True)
+                if not fresh:
+                    fades.append(jnp.exp2(top[i] - peak))
+                    mass += total[i] * fades[i]
+                top[i], total[i] = peak, mass
+                weights.append(weight.astype(jnp.bfloat16))
+            product = jnp.dot(
+                jnp.concatenate(weights, axis=0),
+                v_ref[j * keys : (j + 1) * keys],
+                preferred_element_type=jnp.float32,
+            )
+            for i in range(STEP_HEADS):
+                result[i] = product[parts[i]] + (0.0 if fresh else result[i] * fades[i])
+            scores = coming
+        for i, span in enumerate(spans):
+            if first:
+                top_ref[:, span] = jnp.broadcast_to(top[i], (rows, HEAD_WIDTH))
+                total_ref[:, span] = jnp.broadcast_to(total[i], (rows, HEAD_WIDTH))
+                result_ref[:, span] = result[i]
+            else:
+                out_ref[:, span] = (result[i] / total[i]).astype(out_ref.dtype)
+
+
+def attend(queries, keys, values, key_pos, limit, state=()):
     rows, width = queries.shape
-    heads, count = width // HEAD_WIDTH, key_pos.shape[1]
-    wide = STEP_HEADS * HEAD_WIDTH
-    whole = lambda a: pl.BlockSpec(a.shape, lambda h: (0, 0))
-    return pl.pallas_call(
-        attend_kernel,
-        grid=(width // wide,),
-        in_specs=[
-            pl.BlockSpec((rows, wide), lambda h: (0, h)),
-            whole(keys),
-            whole(values),
-            whole(kv_other),
-            whole(key_pos),
-            whole(limit),
-        ],
-        out_specs=pl.BlockSpec((rows, wide), lambda h: (0, h)),
-        out_shape=jax.ShapeDtypeStruct((rows, width), jnp.bfloat16),
+    count = keys.shape[0]
+    running = jax.ShapeDtypeStruct((rows, width), jnp.float32)
+    return pl.pallas_call(
+        functools.partial(attend_kernel, not state),
+        in_specs=[VMEM] * (5 + len(state)),
+        out_specs=VMEM if state else (VMEM,) * 3,
+        out_shape=jax.ShapeDtypeStruct((rows, width), jnp.bfloat16) if state else (running,) * 3,
         scratch_shapes=[pltpu.VMEM((rows, count), jnp.float32)],
         compiler_params=pltpu.CompilerParams(vmem_limit_bytes=32 << 20),
         cost_estimate=pl.CostEstimate(
             flops=4 * rows * width * count,
             bytes_accessed=4 * rows * width + 4 * count * HEAD_WIDTH,
-            transcendentals=rows * heads * count,
-        ),
-    )(queries, keys, values, kv_other, key_pos, limit)
+            transcendentals=rows * count * width // HEAD_WIDTH,
+        ),
+    )(queries, keys, values, key_pos, limit, *state)
 
 
 def project_kernel(a_ref, w_ref, out_ref):
@@ -127,7 +133,7 @@
     )(both, weights)
 
 
-def add_kernel(parts_ref, residual_ref, hidden_ref, square_ref):
+def add_kernel(parts_ref, residual_ref, hidden_ref, twin_ref, square_ref):
     shares, rows, columns = parts_ref.shape
     squares = []
     for j in range(columns // HEAD_WIDTH):
@@ -139,6 +145,7 @@
                 total += parts_ref[s, :, at].astype(jnp.float32)
             hidden = (residual_ref[:, span].astype(jnp.float32) + total).astype(jnp.bfloat16)
             hidden_ref[:, span] = hidden
+            twin_ref[:, span] = hidden
             wide = hidden.astype(jnp.float32)
             squares.append(wide * wide)
     copies = square_ref.shape[0]
@@ -156,8 +163,9 @@
     return pl.pallas_call(
         add_kernel,
         in_specs=[VMEM, VMEM],
-        out_specs=(VMEM, VMEM),
+        out_specs=(VMEM, VMEM, VMEM),
         out_shape=(
+            jax.ShapeDtypeStruct(shape, jnp.bfloat16),
             jax.ShapeDtypeStruct(shape, jnp.bfloat16),
             jax.ShapeDtypeStruct((nx, shape[0]), jnp.float32),
         ),
@@ -211,25 +219,24 @@
     inner = jnp.arange(half_rows, dtype=jnp.int32)
     table = (half_order[:, None] * half_rows + inner[None, :]).reshape(chips, 2, tok_rows)
     of_core = [table[:, 0].reshape(1, -1), table[:, 1].reshape(1, -1)]
-    key_pos = jnp.where(
-        core == 0,
-        jnp.concatenate(of_core, axis=1),
-        jnp.concatenate(of_core[::-1], axis=1),
-    )
+    pos_own = jnp.where(core == 0, of_core[0], of_core[1])
+    pos_other = jnp.where(core == 0, of_core[1], of_core[0])
     chosen = (jnp.arange(2 * chips, dtype=jnp.int32) == 2 * z + core)[:, None]
     query_pos = jnp.sum(jnp.where(chosen, table.reshape(2 * chips, tok_rows), 0), axis=0)
     frame_starts = jnp.cumsum(frame_lengths) - frame_lengths
     limit = jnp.sum(
         jnp.where(frame_starts[None, :] <= query_pos[:, None], frame_lengths[None, :], 0), axis=1
     )[:, None]
-    attended = attend(queries, k_own, v_own, kv_other, key_pos, limit)
+    state = attend(queries, k_own, v_own, pos_own, limit)
+    k_other, v_other = kv_other[: k_own.shape[0]], kv_other[k_own.shape[0] :]
+    attended = attend(queries, k_other, v_other, pos_other, limit, state)
 
     both = lax.all_gather(attended, "sub", tiled=True)
     parts = project(both, weights, nx).reshape(2 * nx, tok_rows, -1)
     parts = lax.all_to_all(parts, ("heads", "sub"), 0, 0, tiled=True)
-    hidden_state, squares = add_residual(parts, residual_in, nx)
+    hidden_state, twin, squares = add_residual(parts, residual_in, nx)
     squares = lax.all_to_all(squares, "heads", 0, 0, tiled=True)
-    normed = normalise(squares, hidden_state, norm_gain, features)
+    normed = normalise(squares, twin, norm_gain, features)
     return (attended, hidden_state, normed)
 
 

time: 188 us -> 190 us (1.011)
  Pallas kernels: 12.1 us -> 16.7 us
    pallas_call x2 -> x3, Pallas kernels: 8.07 us -> 12.7 us  [the longest x2 11.9 us: attend(): pl.pallas_call(functools.partial(attend_kernel, not state), in_specs=[VME...]
  transfers between devices with their start and end apart: 2 -> 2, of which waited for: 1 -> 0; matrix products, arithmetic and copies ran while one was open for 1% -> 1% of each run, Pallas kernels for 4% -> 6%
where the time goes in v4:
time: 190 us
  blocking collectives  155 us (82%)
  Pallas kernels  16.7 us (9%)
  between operations  14.2 us (7%)
  starting transfers between devices  2.01 us (1%)
    all_gather x1, blocking collectives, shards(): k_own = lax.all_gather(keys, 'seq', tiled=True)  72.3 us
    all_to_all x1, blocking collectives, shards(): parts = lax.all_to_all(parts, ('heads', 'sub'), 0, 0, tiled=True)  34.4 us
    all_gather x1, blocking collectives, shards(): v_own = lax.all_gather(values, 'seq', tiled=True)  34.2 us
    pallas_call x2, Pallas kernels, attend(): pl.pallas_call(functools.partial(attend_kernel, not state), in_specs=[VME...  11.9 us
    all_to_all x1, blocking collectives, shards(): squares = lax.all_to_all(squares, 'heads', 0, 0, tiled=True)  11.6 us
  transfers between devices with their start and end apart: 2, of which 0 were waited for; matrix products, arithmetic and copies ran while one was open for 1% of the time, Pallas kernels for 6%

profile of v4, /device:TPU:80, one launch (start us, length us, event | category | flops | bytes accessed | tf_op | source)
XLA Modules:
  0.0 190.2 jit_solution(9332713794309159631)
XLA Ops:
  7.2 0.1 all-gather.3.cloned.1.call-start
  7.3 0.7 all-gather.3.cloned.1.call-update
  8.0 72.3 %all_gather.15.k_ref = bf16[2048,128]{1,0:T(8,128)(2,1)S(1)} all-gather(bf16[128,128]{1,0:T(8,128)(2,1)} %param.9), channel_id=1, replica_groups=mesh['groups'=2,'seq'=16,'heads'=8,'sub'=2] {'seq'}, dimensions={0}, use_global_device_ids=true | all-gather | bytes 557056 | tf_op jit(solution)/shard_map/all_gather | solution.py:215
  80.3 34.2 %all_gather.16.v_ref = bf16[2048,128]{1,0:T(8,128)(2,1)S(1)} all-gather(bf16[128,128]{1,0:T(8,128)(2,1)} %param.10), channel_id=1, replica_groups=mesh['groups'=2,'seq'=16,'heads'=8,'sub'=2] {'seq'}, dimensions={0}, use_global_device_ids=true | all-gather | bytes 557056 | tf_op jit(solution)/shard_map/all_gather | solution.py:216
  114.6 0.1 pad_maximum_fusion
  114.6 2.0 %collective-permute-start = (bf16[4096,128]{1,0:T(8,128)(2,1)S(1)}, bf16[4096,128]{1,0:T(8,128)(2,1)S(1)}, u32[]{:S(2)}, u32[]{:S(2)}) collective-permute-start(bf16[4096,128]{1,0:T(8,128)(2,1)S(1)} %pad_maximum_fusion), channel_id=1, source_target_pairs={{0,1},{1,0},{2,3},{3,2},{4,5},{5,4},{6,7},{7,6},{8,9},{9,8},{10,11... | collective-permute-start | bytes 3145736 | tf_op jit(solution)/shard_map/ppermute | solution.py:18
  116.6 0.1 add.43
  116.7 0.1 add.35
  116.9 0.1 copy.26
  116.9 0.1 select_reduce_fusion
  117.0 0.1 le.16
  117.1 0.1 copy.25
  117.2 0.1 reduce-window.9
  117.3 0.1 reduce.1
  117.4 0.1 select_reduce_fusion.1
  117.5 0.1 copy.28.limit_ref
  117.6 0.1 add.36
  117.7 0.1 add.37
  117.8 0.1 add.39
  117.9 0.0 copy-done.2
  117.9 3.3 %shard_map.103 = (f32[128,1024]{1,0:T(8,128)S(1)}, f32[128,1024]{1,0:T(8,128)S(1)}, f32[128,1024]{1,0:T(8,128)S(1)}) custom-call(bf16[128,1024]{1,0:T(8,128)(2,1)S(1)} %copy-done.2, bf16[2048,128]{1,0:T(8,128)(2,1)S(1)} %all_gather.15.k_ref, bf16[2048,128]{1,0:T(8,128)(2,1)S(1)} %all_gather.16.v_ref, s32[1,2048]{1,0:T(1,128)S(1)} %bitcast.16, ...), custom_call_target="tpu_custom_call" | custom-call | flops 1073741824 | bytes 1572864 | tf_op jit(solution)/shard_map/pallas_call | solution.py:90
  121.2 0.0 collective-permute-done
  121.3 0.1 fusion
  121.3 8.5 %shard_map.104 = bf16[128,1024]{1,0:T(8,128)(2,1)} custom-call(bf16[128,1024]{1,0:T(8,128)(2,1)S(1)} %copy-done.2, bf16[2048,128]{1,0:T(8,128)(2,1)S(1)} %get-tuple-element.16.k_ref, bf16[2048,128]{1,0:T(8,128)(2,1)S(1)} %get-tuple-element.15.v_ref, s32[1,2048]{1,0:T(1,128)S(1)} %bitcast.15, s32[128,1]{1,0:T(8,128)S(1)} %copy.28.limit_ref, ...), custom_call_target="tpu_custom_call" | custom-call | flops 1073741824 | bytes 1572864 | tf_op jit(solution)/shard_map/pallas_call | solution.py:90
  129.9 2.5 %all_gather.17.a_ref = bf16[256,1024]{1,0:T(8,128)(2,1)S(1)} all-gather(bf16[128,1024]{1,0:T(8,128)(2,1)} %shard_map.104), channel_id=1, replica_groups=mesh['groups'=2,'seq'=16,'heads'=8,'sub'=2] {'sub'}, dimensions={0}, use_global_device_ids=true | all-gather | bytes 786432 | tf_op jit(solution)/shard_map/all_gather | solution.py:234
  132.4 3.0 %shard_map.105 = bf16[8,2,128,256]{3,2,1,0:T(8,128)(2,1)S(1)} custom-call(bf16[256,1024]{1,0:T(8,128)(2,1)S(1)} %all_gather.17.a_ref, bf16[16,1024,128]{2,1,0:T(8,128)(2,1)} %bitcast.19), custom_call_target="tpu_custom_call" | custom-call | flops 1073741824 | bytes 4194304 | tf_op jit(solution)/shard_map/pallas_call | solution.py:118
  135.4 0.0 copy-start
  135.5 0.0 copy-start.1
  135.5 34.4 %all_to_all.16.parts_ref = bf16[16,128,256]{2,1,0:T(8,128)(2,1)S(1)} all-to-all(bf16[16,128,256]{2,1,0:T(8,128)(2,1)S(1)} %bitcast.13), channel_id=1, replica_groups=mesh['groups'=2,'seq'=16,'heads'=8,'sub'=2] {'heads','sub'}, dimensions={0} | all-to-all | bytes 2097152 | tf_op jit(solution)/shard_map/all_to_all | solution.py:236
  169.9 0.8 shard_map.106
  170.7 11.6 %all_to_all.17 = f32[8,1,128]{2,1,0:T(1,128)S(1)} all-to-all(f32[8,1,128]{2,1,0:T(1,128)S(1)} %bitcast.17), channel_id=1, replica_groups=mesh['groups'=2,'seq'=16,'heads'=8,'sub'=2] {'heads'}, dimensions={0} | all-to-all | bytes 8192 | tf_op jit(solution)/shard_map/all_to_all | solution.py:238
  182.4 0.9 shard_map.107
  (15 shorter events, 0.1 us)
Async XLA Ops:
  7.2 109.4 %copy-start.4 = (s32[64]{0:T(128)S(1)}, s32[64]{0:T(128)}, u32[]{:S(2)}) copy-start(s32[64]{0:T(128)} %param.11) | copy-start | bytes 772
  7.2 109.9 %copy-start.3 = (s32[32]{0:T(128)S(1)}, s32[32]{0:T(128)}, u32[]{:S(2)}) copy-start(s32[32]{0:T(128)} %param.12) | copy-start | bytes 388
  7.2 110.7 %copy-start.2 = (bf16[128,1024]{1,0:T(8,128)(2,1)S(1)}, bf16[128,1024]{1,0:T(8,128)(2,1)}, u32[]{:S(2)}) copy-start(bf16[128,1024]{1,0:T(8,128)(2,1)} %q_ref.3) | copy-start | bytes 786436
  7.2 125.2 %all-gather.3.cloned.1.call-start = ((), (), s32[]{:S(2)}) async-start(), calls=%async_computation.2 | async-start | bytes 4456448 | tf_op jit(solution)/shard_map/all_gather | solution.py:214
  114.6 6.6 %collective-permute-start = (bf16[4096,128]{1,0:T(8,128)(2,1)S(1)}, bf16[4096,128]{1,0:T(8,128)(2,1)S(1)}, u32[]{:S(2)}, u32[]{:S(2)}) collective-permute-start(bf16[4096,128]{1,0:T(8,128)(2,1)S(1)} %pad_maximum_fusion), channel_id=1, source_target_pairs={{0,1},{1,0},{2,3},{3,2},{4,5},{5,4},{6,7},{7,6},{8,9},{9,8},{10,11... | collective-permute-start | bytes 3145736 | tf_op jit(solution)/shard_map/ppermute | solution.py:18
  135.4 34.5 %copy-start = (bf16[128,512]{1,0:T(8,128)(2,1)S(1)}, bf16[128,512]{1,0:T(8,128)(2,1)}, u32[]{:S(2)}) copy-start(bf16[128,512]{1,0:T(8,128)(2,1)} %residual_ref.1) | copy-start | bytes 393220
  135.5 46.9 %copy-start.1 = (f32[512]{0:T(512)S(1)}, f32[512]{0:T(512)}, u32[]{:S(2)}) copy-start(f32[512]{0:T(512)} %param.15) | copy-start | bytes 6148
Sparse Core Ops, SparseCore 0:
  10.1 115.4 all-gather.2

commit v5 on v4

--- a/solution.py
+++ b/solution.py
@@ -48,8 +48,8 @@
         if first:
             top, total, result = ([None] * STEP_HEADS for _ in range(3))
         else:
-            top = [top_in[:, span][:, :1] for span in spans]
-            total = [total_in[:, span][:, :1] for span in spans]
+            top = [jnp.max(top_in[:, span], axis=-1, keepdims=True) for span in spans]
+            total = [jnp.max(total_in[:, span], axis=-1, keepdims=True) for span in spans]
             result = [result_in[:, span] for span in spans]
         for j in range(STRETCHES):
             coming = scored(j + 1) if j + 1 < STRETCHES else None

time: 190 us -> 186 us (0.979)
  Pallas kernels: 16.7 us -> 12.5 us
    pallas_call x2, Pallas kernels: 11.9 us -> 7.65 us  [attend(): pl.pallas_call(functools.partial(attend_kernel, not state), in_specs=[VME...]
  transfers between devices with their start and end apart: 2 -> 2, of which waited for: 0 -> 0; matrix products, arithmetic and copies ran while one was open for 1% -> 1% of each run, Pallas kernels for 6% -> 4%
where the time goes in v5:
time: 186 us
  blocking collectives  155 us (83%)
  between operations  14.2 us (8%)
  Pallas kernels  12.5 us (7%)
  starting transfers between devices  2.01 us (1%)
    all_gather x1, blocking collectives, shards(): k_own = lax.all_gather(keys, 'seq', tiled=True)  72.3 us
    all_to_all x1, blocking collectives, shards(): parts = lax.all_to_all(parts, ('heads', 'sub'), 0, 0, tiled=True)  34.5 us
    all_gather x1, blocking collectives, shards(): v_own = lax.all_gather(values, 'seq', tiled=True)  34.2 us
    all_to_all x1, blocking collectives, shards(): squares = lax.all_to_all(squares, 'heads', 0, 0, tiled=True)  11.6 us
    pallas_call x2, Pallas kernels, attend(): pl.pallas_call(functools.partial(attend_kernel, not state), in_specs=[VME...  7.65 us
  transfers between devices with their start and end apart: 2, of which 0 were waited for; matrix products, arithmetic and copies ran while one was open for 1% of the time, Pallas kernels for 4%

profile of v5, /device:TPU:80, one launch (start us, length us, event | category | flops | bytes accessed | tf_op | source)
XLA Modules:
  0.0 186.0 jit_solution(5833973219050134346)
XLA Ops:
  7.2 0.1 all-gather.3.cloned.1.call-start
  7.3 0.7 all-gather.3.cloned.1.call-update
  8.0 72.3 %all_gather.15.k_ref = bf16[2048,128]{1,0:T(8,128)(2,1)S(1)} all-gather(bf16[128,128]{1,0:T(8,128)(2,1)} %param.9), channel_id=1, replica_groups=mesh['groups'=2,'seq'=16,'heads'=8,'sub'=2] {'seq'}, dimensions={0}, use_global_device_ids=true | all-gather | bytes 557056 | tf_op jit(solution)/shard_map/all_gather | solution.py:215
  80.3 34.2 %all_gather.16.v_ref = bf16[2048,128]{1,0:T(8,128)(2,1)S(1)} all-gather(bf16[128,128]{1,0:T(8,128)(2,1)} %param.10), channel_id=1, replica_groups=mesh['groups'=2,'seq'=16,'heads'=8,'sub'=2] {'seq'}, dimensions={0}, use_global_device_ids=true | all-gather | bytes 557056 | tf_op jit(solution)/shard_map/all_gather | solution.py:216
  114.6 0.1 pad_maximum_fusion
  114.6 2.0 %collective-permute-start = (bf16[4096,128]{1,0:T(8,128)(2,1)S(1)}, bf16[4096,128]{1,0:T(8,128)(2,1)S(1)}, u32[]{:S(2)}, u32[]{:S(2)}) collective-permute-start(bf16[4096,128]{1,0:T(8,128)(2,1)S(1)} %pad_maximum_fusion), channel_id=1, source_target_pairs={{0,1},{1,0},{2,3},{3,2},{4,5},{5,4},{6,7},{7,6},{8,9},{9,8},{10,11... | collective-permute-start | bytes 3145736 | tf_op jit(solution)/shard_map/ppermute | solution.py:18
  116.6 0.1 add.43
  116.7 0.1 add.35
  116.9 0.1 copy.26
  116.9 0.1 select_reduce_fusion
  117.0 0.1 le.16
  117.1 0.1 copy.25
  117.2 0.1 reduce-window.9
  117.3 0.1 reduce.1
  117.4 0.1 select_reduce_fusion.1
  117.5 0.1 copy.28.limit_ref
  117.6 0.1 add.36
  117.7 0.1 add.37
  117.8 0.1 add.39
  117.9 3.3 %shard_map.103 = (f32[128,1024]{1,0:T(8,128)S(1)}, f32[128,1024]{1,0:T(8,128)S(1)}, f32[128,1024]{1,0:T(8,128)S(1)}) custom-call(bf16[128,1024]{1,0:T(8,128)(2,1)S(1)} %copy-done.2, bf16[2048,128]{1,0:T(8,128)(2,1)S(1)} %all_gather.15.k_ref, bf16[2048,128]{1,0:T(8,128)(2,1)S(1)} %all_gather.16.v_ref, s32[1,2048]{1,0:T(1,128)S(1)} %bitcast.16, ...), custom_call_target="tpu_custom_call" | custom-call | flops 1073741824 | bytes 1572864 | tf_op jit(solution)/shard_map/pallas_call | solution.py:90
  121.2 0.0 collective-permute-done
  121.3 0.1 fusion
  121.3 4.3 %shard_map.104 = bf16[128,1024]{1,0:T(8,128)(2,1)} custom-call(bf16[128,1024]{1,0:T(8,128)(2,1)S(1)} %copy-done.2, bf16[2048,128]{1,0:T(8,128)(2,1)S(1)} %get-tuple-element.16.k_ref, bf16[2048,128]{1,0:T(8,128)(2,1)S(1)} %get-tuple-element.15.v_ref, s32[1,2048]{1,0:T(1,128)S(1)} %bitcast.15, s32[128,1]{1,0:T(8,128)S(1)} %copy.28.limit_ref, ...), custom_call_target="tpu_custom_call" | custom-call | flops 1073741824 | bytes 1572864 | tf_op jit(solution)/shard_map/pallas_call | solution.py:90
  125.6 2.5 %all_gather.17.a_ref = bf16[256,1024]{1,0:T(8,128)(2,1)S(1)} all-gather(bf16[128,1024]{1,0:T(8,128)(2,1)} %shard_map.104), channel_id=1, replica_groups=mesh['groups'=2,'seq'=16,'heads'=8,'sub'=2] {'sub'}, dimensions={0}, use_global_device_ids=true | all-gather | bytes 786432 | tf_op jit(solution)/shard_map/all_gather | solution.py:234
  128.2 3.0 %shard_map.105 = bf16[8,2,128,256]{3,2,1,0:T(8,128)(2,1)S(1)} custom-call(bf16[256,1024]{1,0:T(8,128)(2,1)S(1)} %all_gather.17.a_ref, bf16[16,1024,128]{2,1,0:T(8,128)(2,1)} %bitcast.19), custom_call_target="tpu_custom_call" | custom-call | flops 1073741824 | bytes 4194304 | tf_op jit(solution)/shard_map/pallas_call | solution.py:118
  131.2 0.0 copy-start
  131.2 0.0 copy-start.1
  131.3 34.5 %all_to_all.16.parts_ref = bf16[16,128,256]{2,1,0:T(8,128)(2,1)S(1)} all-to-all(bf16[16,128,256]{2,1,0:T(8,128)(2,1)S(1)} %bitcast.13), channel_id=1, replica_groups=mesh['groups'=2,'seq'=16,'heads'=8,'sub'=2] {'heads','sub'}, dimensions={0} | all-to-all | bytes 2097152 | tf_op jit(solution)/shard_map/all_to_all | solution.py:236
  165.7 0.8 shard_map.106
  166.5 11.6 %all_to_all.17 = f32[8,1,128]{2,1,0:T(1,128)S(1)} all-to-all(f32[8,1,128]{2,1,0:T(1,128)S(1)} %bitcast.17), channel_id=1, replica_groups=mesh['groups'=2,'seq'=16,'heads'=8,'sub'=2] {'heads'}, dimensions={0} | all-to-all | bytes 8192 | tf_op jit(solution)/shard_map/all_to_all | solution.py:238
  178.2 0.0 copy-done.1
  178.2 0.9 shard_map.107
  (15 shorter events, 0.1 us)
Async XLA Ops:
  7.2 109.4 %copy-start.4 = (s32[64]{0:T(128)S(1)}, s32[64]{0:T(128)}, u32[]{:S(2)}) copy-start(s32[64]{0:T(128)} %param.11) | copy-start | bytes 772
  7.2 109.9 %copy-start.3 = (s32[32]{0:T(128)S(1)}, s32[32]{0:T(128)}, u32[]{:S(2)}) copy-start(s32[32]{0:T(128)} %param.12) | copy-start | bytes 388
  7.2 110.7 %copy-start.2 = (bf16[128,1024]{1,0:T(8,128)(2,1)S(1)}, bf16[128,1024]{1,0:T(8,128)(2,1)}, u32[]{:S(2)}) copy-start(bf16[128,1024]{1,0:T(8,128)(2,1)} %q_ref.3) | copy-start | bytes 786436
  7.2 121.0 %all-gather.3.cloned.1.call-start = ((), (), s32[]{:S(2)}) async-start(), calls=%async_computation.2 | async-start | bytes 4456448 | tf_op jit(solution)/shard_map/all_gather | solution.py:214
  114.6 6.6 %collective-permute-start = (bf16[4096,128]{1,0:T(8,128)(2,1)S(1)}, bf16[4096,128]{1,0:T(8,128)(2,1)S(1)}, u32[]{:S(2)}, u32[]{:S(2)}) collective-permute-start(bf16[4096,128]{1,0:T(8,128)(2,1)S(1)} %pad_maximum_fusion), channel_id=1, source_target_pairs={{0,1},{1,0},{2,3},{3,2},{4,5},{5,4},{6,7},{7,6},{8,9},{9,8},{10,11... | collective-permute-start | bytes 3145736 | tf_op jit(solution)/shard_map/ppermute | solution.py:18
  131.2 34.5 %copy-start = (bf16[128,512]{1,0:T(8,128)(2,1)S(1)}, bf16[128,512]{1,0:T(8,128)(2,1)}, u32[]{:S(2)}) copy-start(bf16[128,512]{1,0:T(8,128)(2,1)} %residual_ref.1) | copy-start | bytes 393220
  131.2 46.9 %copy-start.1 = (f32[512]{0:T(512)S(1)}, f32[512]{0:T(512)}, u32[]{:S(2)}) copy-start(f32[512]{0:T(512)} %param.15) | copy-start | bytes 6148
Sparse Core Ops, SparseCore 0:
  10.1 115.4 all-gather.2

commit v6 on v5

--- a/solution.py
+++ b/solution.py
@@ -133,17 +133,34 @@
     )(both, weights)
 
 
-def add_kernel(parts_ref, residual_ref, hidden_ref, twin_ref, square_ref):
-    shares, rows, columns = parts_ref.shape
+def sum_kernel(parts_ref, out_ref):
+    total = parts_ref[0].astype(jnp.float32)
+    for s in range(1, parts_ref.shape[0]):
+        total += parts_ref[s].astype(jnp.float32)
+    out_ref[...] = total
+
+
+def sum_shares(parts):
+    return pl.pallas_call(
+        sum_kernel,
+        in_specs=[VMEM],
+        out_specs=VMEM,
+        out_shape=jax.ShapeDtypeStruct(parts.shape[1:], jnp.float32),
+        compiler_params=pltpu.CompilerParams(vmem_limit_bytes=8 << 20),
+        cost_estimate=pl.CostEstimate(
+            flops=2 * parts.size, bytes_accessed=2 * parts.size, transcendentals=0
+        ),
+    )(parts)
+
+
+def add_kernel(sums_ref, residual_ref, hidden_ref, twin_ref, square_ref):
     squares = []
-    for j in range(columns // HEAD_WIDTH):
+    for j in range(sums_ref.shape[2] // HEAD_WIDTH):
         at = slice(j * HEAD_WIDTH, (j + 1) * HEAD_WIDTH)
         for c in range(2):
             span = slice((2 * j + c) * HEAD_WIDTH, (2 * j + c + 1) * HEAD_WIDTH)
-            total = parts_ref[c, :, at].astype(jnp.float32)
-            for s in range(2 + c, shares, 2):
-                total += parts_ref[s, :, at].astype(jnp.float32)
-            hidden = (residual_ref[:, span].astype(jnp.float32) + total).astype(jnp.bfloat16)
+            total = residual_ref[:, span].astype(jnp.float32) + sums_ref[c, :, at]
+            hidden = total.astype(jnp.bfloat16)
             hidden_ref[:, span] = hidden
             twin_ref[:, span] = hidden
             wide = hidden.astype(jnp.float32)
@@ -158,7 +175,7 @@
     )
 
 
-def add_residual(parts, residual, nx):
+def add_residual(sums, residual, nx):
     shape = residual.shape
     return pl.pallas_call(
         add_kernel,
@@ -171,9 +188,9 @@
         ),
         compiler_params=pltpu.CompilerParams(vmem_limit_bytes=8 << 20),
         cost_estimate=pl.CostEstimate(
-            flops=2 * parts.size, bytes_accessed=2 * parts.size, transcendentals=0
-        ),
-    )(parts, residual)
+            flops=4 * sums.size, bytes_accessed=4 * sums.size, transcendentals=0
+        ),
+    )(sums, residual)
 
 
 def norm_kernel(features, square_ref, hidden_ref, gain_ref, out_ref):
@@ -232,9 +249,10 @@
     attended = attend(queries, k_other, v_other, pos_other, limit, state)
 
     both = lax.all_gather(attended, "sub", tiled=True)
-    parts = project(both, weights, nx).reshape(2 * nx, tok_rows, -1)
-    parts = lax.all_to_all(parts, ("heads", "sub"), 0, 0, tiled=True)
-    hidden_state, twin, squares = add_residual(parts, residual_in, nx)
+    parts = project(both, weights, nx).reshape(nx, 2 * tok_rows, -1)
+    sums = sum_shares(lax.all_to_all(parts, "heads", 0, 0, tiled=True))
+    sums = lax.all_to_all(sums.reshape(2, tok_rows, -1), "sub", 0, 0, tiled=True)
+    hidden_state, twin, squares = add_residual(sums, residual_in, nx)
     squares = lax.all_to_all(squares, "heads", 0, 0, tiled=True)
     normed = normalise(squares, twin, norm_gain, features)
     return (attended, hidden_state, normed)

time: 186 us -> 191 us (1.027)
  blocking collectives: 155 us -> 160 us
    all_to_all x1 -> x2, blocking collectives: 34.5 us -> 40.4 us  [the longest x1 36.4 us: shards(): sums = sum_shares(lax.all_to_all(parts, 'heads', 0, 0, tiled=True))]
where the time goes in v6:
time: 191 us; the launch traced here: 190 us
  blocking collectives  160 us (84%)
  between operations  14.2 us (7%)
  Pallas kernels  12.5 us (7%)
  starting transfers between devices  2.01 us (1%)
    all_gather x1, blocking collectives, shards(): k_own = lax.all_gather(keys, 'seq', tiled=True)  72.3 us
    all_to_all x1, blocking collectives, shards(): sums = sum_shares(lax.all_to_all(parts, 'heads', 0, 0, tiled=True))  36.4 us
    all_gather x1, blocking collectives, shards(): v_own = lax.all_gather(values, 'seq', tiled=True)  34.2 us
    all_to_all x1, blocking collectives, shards(): squares = lax.all_to_all(squares, 'heads', 0, 0, tiled=True)  10.1 us
    pallas_call x2, Pallas kernels, attend(): pl.pallas_call(functools.partial(attend_kernel, not state), in_specs=[VME...  7.65 us
    all_to_all x1, blocking collectives, shards(): lax.all_to_all(sums.reshape(2, tok_rows, -1), 'sub', 0, 0, tiled=True)  3.96 us
  transfers between devices with their start and end apart: 2, of which 0 were waited for; matrix products, arithmetic and copies ran while one was open for 1% of the time, Pallas kernels for 4%

profile of v6, /device:TPU:80, one launch (start us, length us, event | category | flops | bytes accessed | tf_op | source)
XLA Modules:
  0.0 190.4 jit_solution(17288646407606101435)
XLA Ops:
  7.2 0.1 all-gather.3.cloned.1.call-start
  7.3 0.7 all-gather.3.cloned.1.call-update
  8.0 72.3 %all_gather.15.k_ref = bf16[2048,128]{1,0:T(8,128)(2,1)S(1)} all-gather(bf16[128,128]{1,0:T(8,128)(2,1)} %param.9), channel_id=1, replica_groups=mesh['groups'=2,'seq'=16,'heads'=8,'sub'=2] {'seq'}, dimensions={0}, use_global_device_ids=true | all-gather | bytes 557056 | tf_op jit(solution)/shard_map/all_gather | solution.py:232
  80.3 34.2 %all_gather.16.v_ref = bf16[2048,128]{1,0:T(8,128)(2,1)S(1)} all-gather(bf16[128,128]{1,0:T(8,128)(2,1)} %param.10), channel_id=1, replica_groups=mesh['groups'=2,'seq'=16,'heads'=8,'sub'=2] {'seq'}, dimensions={0}, use_global_device_ids=true | all-gather | bytes 557056 | tf_op jit(solution)/shard_map/all_gather | solution.py:233
  114.6 0.1 pad_maximum_fusion
  114.6 2.0 %collective-permute-start = (bf16[4096,128]{1,0:T(8,128)(2,1)S(1)}, bf16[4096,128]{1,0:T(8,128)(2,1)S(1)}, u32[]{:S(2)}, u32[]{:S(2)}) collective-permute-start(bf16[4096,128]{1,0:T(8,128)(2,1)S(1)} %pad_maximum_fusion), channel_id=1, source_target_pairs={{0,1},{1,0},{2,3},{3,2},{4,5},{5,4},{6,7},{7,6},{8,9},{9,8},{10,11... | collective-permute-start | bytes 3145736 | tf_op jit(solution)/shard_map/ppermute | solution.py:18
  116.6 0.1 add.43
  116.7 0.1 add.35
  116.9 0.1 copy.26
  116.9 0.1 select_reduce_fusion
  117.0 0.1 le.16
  117.1 0.1 copy.25
  117.2 0.1 reduce-window.9
  117.3 0.1 reduce.1
  117.4 0.1 select_reduce_fusion.1
  117.5 0.1 copy.28.limit_ref
  117.6 0.1 add.36
  117.7 0.1 add.37
  117.8 0.1 add.39
  117.9 3.3 %shard_map.103 = (f32[128,1024]{1,0:T(8,128)S(1)}, f32[128,1024]{1,0:T(8,128)S(1)}, f32[128,1024]{1,0:T(8,128)S(1)}) custom-call(bf16[128,1024]{1,0:T(8,128)(2,1)S(1)} %copy-done.2, bf16[2048,128]{1,0:T(8,128)(2,1)S(1)} %all_gather.15.k_ref, bf16[2048,128]{1,0:T(8,128)(2,1)S(1)} %all_gather.16.v_ref, s32[1,2048]{1,0:T(1,128)S(1)} %bitcast.18, ...), custom_call_target="tpu_custom_call" | custom-call | flops 1073741824 | bytes 1572864 | tf_op jit(solution)/shard_map/pallas_call | solution.py:90
  121.3 0.1 fusion
  121.3 4.3 %shard_map.104 = bf16[128,1024]{1,0:T(8,128)(2,1)} custom-call(bf16[128,1024]{1,0:T(8,128)(2,1)S(1)} %copy-done.2, bf16[2048,128]{1,0:T(8,128)(2,1)S(1)} %get-tuple-element.16.k_ref, bf16[2048,128]{1,0:T(8,128)(2,1)S(1)} %get-tuple-element.15.v_ref, s32[1,2048]{1,0:T(1,128)S(1)} %bitcast.17, s32[128,1]{1,0:T(8,128)S(1)} %copy.28.limit_ref, ...), custom_call_target="tpu_custom_call" | custom-call | flops 1073741824 | bytes 1572864 | tf_op jit(solution)/shard_map/pallas_call | solution.py:90
  125.6 2.5 %all_gather.17.a_ref = bf16[256,1024]{1,0:T(8,128)(2,1)S(1)} all-gather(bf16[128,1024]{1,0:T(8,128)(2,1)} %shard_map.104), channel_id=1, replica_groups=mesh['groups'=2,'seq'=16,'heads'=8,'sub'=2] {'sub'}, dimensions={0}, use_global_device_ids=true | all-gather | bytes 786432 | tf_op jit(solution)/shard_map/all_gather | solution.py:251
  128.2 3.0 %shard_map.105 = bf16[8,2,128,256]{3,2,1,0:T(8,128)(2,1)S(1)} custom-call(bf16[256,1024]{1,0:T(8,128)(2,1)S(1)} %all_gather.17.a_ref, bf16[16,1024,128]{2,1,0:T(8,128)(2,1)} %bitcast.21), custom_call_target="tpu_custom_call" | custom-call | flops 1073741824 | bytes 4194304 | tf_op jit(solution)/shard_map/pallas_call | solution.py:118
  131.2 0.0 copy-start
  131.2 0.0 copy-start.1
  131.3 36.4 %all_to_all.21.parts_ref = bf16[8,256,256]{2,1,0:T(8,128)(2,1)S(1)} all-to-all(bf16[8,256,256]{2,1,0:T(8,128)(2,1)S(1)} %bitcast.14), channel_id=1, replica_groups=mesh['groups'=2,'seq'=16,'heads'=8,'sub'=2] {'heads'}, dimensions={0} | all-to-all | bytes 2097152 | tf_op jit(solution)/shard_map/all_to_all | solution.py:253
  167.7 0.1 shard_map.106
  167.8 4.0 %all_to_all.22.sums_ref = f32[2,128,256]{2,1,0:T(8,128)S(1)} all-to-all(f32[2,128,256]{2,1,0:T(8,128)S(1)} %bitcast.15), channel_id=1, replica_groups=mesh['groups'=2,'seq'=16,'heads'=8,'sub'=2] {'sub'}, dimensions={0} | all-to-all | bytes 524288 | tf_op jit(solution)/shard_map/all_to_all | solution.py:254
  171.8 0.7 shard_map.107
  172.5 10.1 %all_to_all.23 = f32[8,1,128]{2,1,0:T(1,128)S(1)} all-to-all(f32[8,1,128]{2,1,0:T(1,128)S(1)} %bitcast.19), channel_id=1, replica_groups=mesh['groups'=2,'seq'=16,'heads'=8,'sub'=2] {'heads'}, dimensions={0} | all-to-all | bytes 8192 | tf_op jit(solution)/shard_map/all_to_all | solution.py:256
  182.6 0.9 shard_map.108
  (17 shorter events, 0.1 us)
Async XLA Ops:
  7.2 109.4 %copy-start.4 = (s32[64]{0:T(128)S(1)}, s32[64]{0:T(128)}, u32[]{:S(2)}) copy-start(s32[64]{0:T(128)} %param.11) | copy-start | bytes 772
  7.2 109.9 %copy-start.3 = (s32[32]{0:T(128)S(1)}, s32[32]{0:T(128)}, u32[]{:S(2)}) copy-start(s32[32]{0:T(128)} %param.12) | copy-start | bytes 388
  7.2 110.7 %copy-start.2 = (bf16[128,1024]{1,0:T(8,128)(2,1)S(1)}, bf16[128,1024]{1,0:T(8,128)(2,1)}, u32[]{:S(2)}) copy-start(bf16[128,1024]{1,0:T(8,128)(2,1)} %q_ref.3) | copy-start | bytes 786436
  7.2 121.0 %all-gather.3.cloned.1.call-start = ((), (), s32[]{:S(2)}) async-start(), calls=%async_computation.3 | async-start | bytes 4456448 | tf_op jit(solution)/shard_map/all_gather | solution.py:231
  114.6 6.6 %collective-permute-start = (bf16[4096,128]{1,0:T(8,128)(2,1)S(1)}, bf16[4096,128]{1,0:T(8,128)(2,1)S(1)}, u32[]{:S(2)}, u32[]{:S(2)}) collective-permute-start(bf16[4096,128]{1,0:T(8,128)(2,1)S(1)} %pad_maximum_fusion), channel_id=1, source_target_pairs={{0,1},{1,0},{2,3},{3,2},{4,5},{5,4},{6,7},{7,6},{8,9},{9,8},{10,11... | collective-permute-start | bytes 3145736 | tf_op jit(solution)/shard_map/ppermute | solution.py:18
  131.2 40.6 %copy-start = (bf16[128,512]{1,0:T(8,128)(2,1)S(1)}, bf16[128,512]{1,0:T(8,128)(2,1)}, u32[]{:S(2)}) copy-start(bf16[128,512]{1,0:T(8,128)(2,1)} %residual_ref.1) | copy-start | bytes 393220
  131.2 51.4 %copy-start.1 = (f32[512]{0:T(512)S(1)}, f32[512]{0:T(512)}, u32[]{:S(2)}) copy-start(f32[512]{0:T(512)} %param.15) | copy-start | bytes 6148
Sparse Core Ops, SparseCore 0:
  10.1 115.4 all-gather.2
